TPU v7x, 32 devices: a whole 2x2x4 slice. The times are simulated.
32 devices in a mesh: ctx: 8 (over z, core), head: 4 (over y, x).
Axes of the slice: x: 2, y: 2, z: 4, core: 2. Of those that a mesh axis runs over, the one named last changes fastest.
Arguments:
- stretch_keys: bfloat16 [4, 32768, 128], P('head', 'ctx'), may hold values from -6 to 6
- stretch_values: bfloat16 [4, 32768, 128], P('head', 'ctx'), may hold values from -6 to 6
- stretch_assign: int32 [4, 32768], P('head', 'ctx'), may hold values from 0 to 4095, as said below
- centroid_keys: float32 [4, 4096, 128], P('head'), may hold values from -3.5 to 3.5
- centroid_values: float32 [4, 4096, 128], P('head'), may hold values from -3 to 3
- cluster_counts: float32 [4, 4096], P('head'), may hold values from 64 to 1024
- cache_keys: bfloat16 [4, 65536, 128], P('head', 'ctx'), may hold values from -6 to 6
- cache_values: bfloat16 [4, 65536, 128], P('head', 'ctx'), may hold values from -6 to 6
- block_cluster: int32 [4, 4096], P('head', 'ctx'), may hold values from 0 to 4095
- selected: int32 [4, 4, 64], P(None, 'head'), may hold values from 0 to 4095
- queries: bfloat16 [4, 64, 4, 128], P(None, 'head'), may hold values from -90 to 90
Outputs:
- new_keys: float32 [4, 4096, 128], P('head', 'ctx')
- new_values: float32 [4, 4096, 128], P('head', 'ctx')
- new_counts: float32 [4, 4096], P('head', 'ctx')
- attended: bfloat16 [4, 4, 64, 128], P(None, 'head', 'ctx')
Inputs may be any that keep to these rules, and one draw needn't show every extreme that they name: `stretch_assign`: within each aligned block of 4096 prefill positions of one head, the clusters of one group j // (4096 / 8) are named at most 640 times; in every block some group is named exactly 640 times.
All inputs are finite; a program needn't handle non-finite values.
Results may differ from a plain program's by a relative error of at most 0.0045.
Values may be sent and summed in bfloat16 or wider, within the bound.
No kernel may reach another device: no remote copies, remote signals or barrier semaphores. Data moves between devices by JAX's collectives and lax.ppermute only.
A program may use at most 128 MiB of HBM per device.

v0:
```python
import functools
import math
import jax
import jax.numpy as jnp
from jax import lax
from jax.experimental import pallas as pl
from jax.experimental.pallas import tpu as pltpu
from jax.sharding import PartitionSpec as P


LANES = 128
TAIL = 16
NEG = -1e30
LOG2E = math.log2(math.e)


def vmem(count):
    return [pl.BlockSpec(memory_space=pltpu.VMEM)] * count


def smem(count):
    return [pl.BlockSpec(memory_space=pltpu.SMEM)] * count


def params(mib):
    return pltpu.CompilerParams(vmem_limit_bytes=mib * 2**20)


def cost(flops, moved=2**20):
    return pl.CostEstimate(flops=int(flops), bytes_accessed=int(moved), transcendentals=0)


def turn_body(me_ref, in_ref, *refs):
    outs, held = refs[:-1], refs[-1]
    heads = len(outs)
    held[...] = in_ref[...].astype(jnp.float32)
    for d, out_ref in enumerate(outs):
        head = lax.rem(me_ref[0] + d, heads)
        out_ref[...] = held[pl.ds(head, out_ref.shape[0], stride=heads), :].astype(out_ref.dtype)


def by_head(me, queries):
    steps, rows, heads, width = queries.shape
    return pl.pallas_call(
        turn_body,
        in_specs=smem(1) + vmem(1), out_specs=vmem(heads),
        out_shape=[jax.ShapeDtypeStruct((steps * rows, width), queries.dtype)] * heads,
        scratch_shapes=[pltpu.VMEM((steps * rows * heads, width), jnp.float32)],
        compiler_params=params(4), cost_estimate=cost(1e8),
        name="by_head",
    )(me.reshape(1), queries.reshape(steps * rows * heads, width))


def count_body(mine_ref, other_ref, out_ref, *, rows):
    total = jnp.zeros((rows, LANES), jnp.float32)
    for ref in (mine_ref, other_ref):
        ids = ref[...]
        span = ids.shape[1]
        upper = (ids // LANES).astype(jnp.int16)
        lower = (ids % LANES).astype(jnp.int16)
        high = lax.broadcasted_iota(jnp.int16, (rows, span), 0) == upper
        low = lax.broadcasted_iota(jnp.int16, (LANES, span), 0) == lower
        one, none = jnp.bfloat16(1), jnp.bfloat16(0)
        total = total + lax.dot_general(
            jnp.where(high, one, none), jnp.where(low, one, none),
            (((1,), (1,)), ((), ())), preferred_element_type=jnp.float32,
        )
    out_ref[...] = total


def chip_counts(mine, other, clusters):
    rows = clusters // LANES
    return pl.pallas_call(
        functools.partial(count_body, rows=rows),
        in_specs=vmem(2), out_specs=vmem(1)[0],
        out_shape=jax.ShapeDtypeStruct((rows, LANES), jnp.float32),
        compiler_params=params(8), cost_estimate=cost(1e9),
        name="chip_counts",
    )(mine, other)


def segment_body(slot_ref, *refs, owned, sources, started, counted):
    out_ref = refs[-1]
    base = slot_ref[0] * owned
    parts = [refs[3 * sources][...]] if started else []
    positions = refs[0].shape[0]
    span = min(2048, positions)
    for i in range(sources):
        keys, values, ids = refs[3 * i : 3 * i + 3]
        for at in range(0, positions, span):
            near = (ids[:, at : at + span] - base).astype(jnp.int16)
            spots = lax.broadcasted_iota(jnp.int16, (owned, span), 0)
            hot = jnp.where(spots == near, jnp.bfloat16(1), jnp.bfloat16(0))
            rows = jnp.concatenate([keys[at : at + span, :], values[at : at + span, :]], axis=1)
            parts.append(jnp.dot(hot, rows, preferred_element_type=jnp.float32))
    total = functools.reduce(jnp.add, parts)
    if not counted:
        out_ref[...] = total
        return
    out_ref[:owned, :] = total.astype(out_ref.dtype)
    counts = refs[3 * sources + started][slot_ref[0]]
    high = jnp.floor(counts * (1.0 / 256.0))
    low = counts - 256.0 * high
    lines = counts.shape[0]
    packed = jnp.concatenate([high, low], axis=1)
    packed = jnp.concatenate(
        [packed, jnp.zeros((TAIL - lines, 2 * LANES), jnp.float32)], axis=0
    )
    out_ref[owned:, :] = packed.astype(out_ref.dtype)


def segment_sums(slot, sources, start, counts, owned, dtype):
    positions, width = sources[0][0].shape
    lines = owned // LANES
    args = [slot.reshape(1)]
    for source in sources:
        args += source
    if start is not None:
        args.append(start)
    if counts is not None:
        args.append(counts.reshape(-1, lines, LANES))
    height = owned if counts is None else owned + TAIL
    return pl.pallas_call(
        functools.partial(
            segment_body, owned=owned, sources=len(sources), started=start is not None,
            counted=counts is not None,
        ),
        in_specs=smem(1) + vmem(len(args) - 1), out_specs=vmem(1)[0],
        out_shape=jax.ShapeDtypeStruct((height, 2 * width), dtype),
        compiler_params=params(12),
        cost_estimate=cost(4 * len(sources) * positions * owned * width),
    )(*args)


def relay_body(own_ref, came_ref, out_ref, *, owned, lines):
    out_ref[:owned, :] = (
        own_ref[:owned, :].astype(jnp.float32) + came_ref[:owned, :].astype(jnp.float32)
    ).astype(out_ref.dtype)
    tail_own = own_ref[owned:, :].astype(jnp.float32)
    tail_came = came_ref[owned:, :].astype(jnp.float32)
    out_ref[owned:, :] = jnp.concatenate(
        [tail_own[:lines], tail_came[:lines], tail_own[2 * lines :]], axis=0
    ).astype(out_ref.dtype)


def relay(own, came, owned):
    return pl.pallas_call(
        functools.partial(relay_body, owned=owned, lines=owned // LANES),
        in_specs=vmem(2), out_specs=vmem(1)[0],
        out_shape=jax.ShapeDtypeStruct(own.shape, own.dtype),
        compiler_params=params(8), cost_estimate=cost(1e9),
        name="relay",
    )(own, came)


def dense_body(
    me_ref, *refs, scale, steps, span, block_len, heads
):
    asked = refs[:heads]
    (kc, vc, blocks, ks, vs, ids, sel_ref,
    peak_ref, whole_ref, acc_ref, q_ref, own_ref, query, held, best, sums, cache_bias, near_bias) = refs[heads:]
    rows = q_ref.shape[0] // steps
    piece = rows // heads
    for d, ref in enumerate(asked):
        part = ref[...].astype(jnp.float32)
        source = lax.rem(me_ref[1] + heads - d, heads)
        for s in range(steps):
            at = pl.ds(pl.multiple_of(s * rows + source * piece, piece), piece)
            q_ref[at, :] = part[s * piece : (s + 1) * piece]
    query[...] = q_ref[...].astype(query.dtype)
    chosen = sel_ref.shape[1]
    eye = lax.broadcasted_iota(jnp.int32, (chosen, chosen), 0) == lax.broadcasted_iota(
        jnp.int32, (chosen, chosen), 1
    )
    wanted = [
        jnp.sum(jnp.where(eye, sel_ref[s : s + 1, :].astype(jnp.float32), 0.0), axis=1, keepdims=True)
        for s in range(steps)
    ]

    def hits(names, s):
        same = names.astype(jnp.float32) == wanted[s]
        return jnp.max(jnp.where(same, 1.0, 0.0), axis=0, keepdims=True)

    owned = own_ref.shape[1]
    mine = me_ref[0] * owned + lax.broadcasted_iota(jnp.int32, (1, owned), 1)
    for s in range(steps):
        own_ref[s : s + 1, :] = hits(mine, s) * NEG
        near_bias[s : s + 1, :] = (1.0 - hits(ids[...], s)) * NEG
        cache_bias[s : s + 1, :] = 1.0 - hits(blocks[...], s)

    per = span // block_len
    widen = jnp.where(
        lax.broadcasted_iota(jnp.int32, (per, span), 0)
        == lax.broadcasted_iota(jnp.int32, (per, span), 1) // block_len,
        1.0, 0.0,
    ).astype(jnp.bfloat16)
    best[...] = jnp.full_like(best, NEG)
    sums[...] = jnp.zeros_like(sums)
    acc_ref[...] = jnp.zeros_like(acc_ref)

    def score(keys, at, shift, base):
        found = lax.dot_general(
            query[...], keys[at, :], (((1,), (1,)), ((), ())), preferred_element_type=jnp.float32
        )
        found = found * scale
        found = jnp.concatenate(
            [found[s * rows : (s + 1) * rows] + shift[s : s + 1] for s in range(steps)], axis=0
        )
        held[:, pl.ds(pl.multiple_of(base + at.start, span), span)] = found
        top = best[...]
        for i in range(span // LANES):
            top = jnp.maximum(top, found[:, i * LANES : (i + 1) * LANES])
        best[...] = top

    def window(turn):
        return pl.ds(pl.multiple_of(turn * span, span), span)

    def score_cache(turn, carry):
        shift = cache_bias[:, pl.ds(pl.multiple_of(turn * per, per), per)].astype(jnp.bfloat16)
        shift = jnp.dot(shift, widen, preferred_element_type=jnp.float32) * NEG
        score(kc, window(turn), shift, 0)
        return carry

    def score_near(turn, carry):
        score(ks, window(turn), near_bias[:, window(turn)], kc.shape[0])
        return carry

    lax.fori_loop(0, kc.shape[0] // span, score_cache, 0)
    lax.fori_loop(0, ks.shape[0] // span, score_near, 0)
    peak = jnp.max(best[...], axis=1, keepdims=True)
    peak_ref[...] = peak
    best[...] = jnp.broadcast_to(peak, best.shape)

    def weigh(values, at, base):
        top = best[...]
        total = sums[...]
        pieces = []
        for i in range(span // LANES):
            lanes = pl.ds(pl.multiple_of(base + at.start + i * LANES, LANES), LANES)
            piece = jnp.exp2(held[:, lanes] - top)
            total = total + piece
            pieces.append(piece.astype(jnp.bfloat16))
        sums[...] = total
        acc_ref[...] += jnp.dot(
            jnp.concatenate(pieces, axis=1), values[at, :], preferred_element_type=jnp.float32
        )

    def weigh_cache(turn, carry):
        weigh(vc, window(turn), 0)
        return carry

    def weigh_near(turn, carry):
        weigh(vs, window(turn), kc.shape[0])
        return carry

    lax.fori_loop(0, kc.shape[0] // span, weigh_cache, 0)
    lax.fori_loop(0, ks.shape[0] // span, weigh_near, 0)
    whole_ref[...] = jnp.sum(sums[...], axis=1, keepdims=True)


def dense_part(me, head, asked, cache_k, cache_v, blocks, near_k, near_v, ids, chosen, owned):
    width = asked[0].shape[1]
    heads = len(asked)
    rows = heads * asked[0].shape[0]
    steps = chosen.shape[0]
    far, near = cache_k.shape[0], near_k.shape[0]
    f32 = jnp.float32
    square = jax.ShapeDtypeStruct((rows, width), f32)
    column = jax.ShapeDtypeStruct((rows, 1), f32)
    tile = pltpu.VMEM((rows, LANES), f32)
    return pl.pallas_call(
        functools.partial(
            dense_body, scale=width ** (-0.5) * LOG2E, steps=steps, span=min(2048, far, near),
            block_len=far // blocks.shape[1], heads=heads,
        ),
        in_specs=smem(1) + vmem(heads + 7), out_specs=vmem(5),
        out_shape=[column, column, square, square, jax.ShapeDtypeStruct((steps, owned), f32)],
        scratch_shapes=[
            pltpu.VMEM((rows, width), asked[0].dtype), pltpu.VMEM((rows, far + near), f32), tile, tile,
            pltpu.VMEM((steps, blocks.shape[1]), f32), pltpu.VMEM((steps, near), f32),
        ],
        compiler_params=params(24),
        cost_estimate=cost(4 * rows * (far + near) * width),
        name="dense_part",
    )(jnp.stack([me, head]), *asked, cache_k, cache_v, blocks, near_k, near_v, ids, chosen)


def finish_body(
    me_ref, own_ref, *refs, owned, lines, steps, groups, scale, parcels
):
    came = refs[:parcels]
    (ck, cv, cc, bias_ref, q_ref, peak_ref, whole_ref, acc_ref,
     nk_ref, nv_ref, nc_ref, out_ref, res_ref) = refs[parcels:]
    width = ck.shape[1]
    hp = lax.Precision.HIGHEST
    sums = own_ref[:owned, :]
    tail = own_ref[owned:, :]
    for ref in came:
        sums = sums + ref[:owned, :].astype(jnp.float32)
        tail = tail + ref[owned:, :].astype(jnp.float32)
    pairs = 256.0 * tail[:, :LANES] + tail[:, LANES:]
    added = pairs[:lines] + pairs[lines : 2 * lines]
    old = cc[0]
    total = old + added
    nc_ref[0] = total
    eye = lax.broadcasted_iota(jnp.int32, (LANES, LANES), 0) == lax.broadcasted_iota(
        jnp.int32, (LANES, LANES), 1
    )

    def stand(row):
        return jnp.sum(jnp.where(eye, row, 0.0), axis=1, keepdims=True)

    old_col = jnp.concatenate([stand(old[i : i + 1]) for i in range(lines)], axis=0)
    new_col = jnp.concatenate([stand(total[i : i + 1]) for i in range(lines)], axis=0)
    new_k = (old_col * ck[...] + sums[:, :width]) / new_col
    new_v = (old_col * cv[...] + sums[:, width:]) / new_col
    nk_ref[...] = new_k
    nv_ref[...] = new_v
    logs = jnp.log(total) * LOG2E
    log_row = jnp.concatenate([logs[i : i + 1] for i in range(lines)], axis=1)
    scores = lax.dot_general(
        q_ref[...], new_k, (((1,), (1,)), ((), ())),
        precision=hp, preferred_element_type=jnp.float32,
    )
    scores = scores * scale + log_row
    rows_all = scores.shape[0]
    rows = rows_all // steps
    shift = bias_ref[...]
    scores = jnp.concatenate(
        [scores[s * rows : (s + 1) * rows] + shift[s : s + 1] for s in range(steps)], axis=0
    )
    before = peak_ref[...]
    peak = jnp.maximum(before, jnp.max(scores, axis=1, keepdims=True))
    weights = jnp.exp2(scores - peak)
    fade = jnp.exp2(before - peak)
    whole = whole_ref[...] * fade + jnp.sum(weights, axis=1, keepdims=True)
    acc = acc_ref[...] * fade + jnp.dot(
        weights, new_v, precision=hp, preferred_element_type=jnp.float32
    )
    res_ref[...] = acc / whole
    level = peak + jnp.log(whole) * LOG2E
    marks = [
        jnp.sum(jnp.where(eye, level[i * LANES : (i + 1) * LANES], 0.0), axis=0, keepdims=True)
        for i in range(rows_all // LANES)
    ]
    marks = jnp.concatenate(marks + [jnp.zeros((8 - len(marks), LANES), jnp.float32)], axis=0)
    share = rows // groups
    for g in range(groups):
        for s in range(steps):
            out_ref[g, s * share : (s + 1) * share, :] = res_ref[
                s * rows + g * share : s * rows + (g + 1) * share, :
            ]
        out_ref[g, steps * share :, :] = marks


def finish(me, own, came, cent_k, cent_v, counts, bias, query, dense, groups, owned):
    width = cent_k.shape[1]
    rows = query.shape[0]
    steps = bias.shape[0]
    lines = owned // LANES
    height = steps * (rows // steps // groups) + 8
    f32 = jnp.float32
    args = [me.reshape(1), own, *came, cent_k, cent_v, counts, bias, query, *dense]
    return pl.pallas_call(
        functools.partial(
            finish_body, owned=owned, lines=lines, steps=steps, groups=groups,
            scale=width ** (-0.5) * LOG2E, parcels=len(came),
        ),
        in_specs=smem(1) + vmem(len(args) - 1), out_specs=vmem(4),
        scratch_shapes=[pltpu.VMEM((rows, width), f32)],
        out_shape=[
            jax.ShapeDtypeStruct((owned, width), f32),
            jax.ShapeDtypeStruct((owned, width), f32),
            jax.ShapeDtypeStruct((1, lines, LANES), f32),
            jax.ShapeDtypeStruct((groups, height, LANES), f32),
        ],
        compiler_params=params(16), cost_estimate=cost(4e9),
        name="finish",
    )(*args)


def blend_body(me_ref, in_ref, out_ref, *, steps, share, groups, rows):
    count = steps * share
    tiles = steps * rows // LANES
    spot = lax.broadcasted_iota(jnp.int32, (count, LANES), 0)
    lane = lax.broadcasted_iota(jnp.int32, (count, LANES), 1)
    wanted = (spot // share) * rows + me_ref[0] * share + spot % share
    picks = [wanted == lane + i * LANES for i in range(tiles)]
    levels = []
    for g in range(groups):
        level = jnp.zeros((count, LANES), jnp.float32)
        for i in range(tiles):
            level = level + jnp.where(picks[i], in_ref[g, count + i : count + i + 1, :], 0.0)
        levels.append(jnp.sum(level, axis=1, keepdims=True))
    top = functools.reduce(jnp.maximum, levels)
    parts = [jnp.exp2(level - top) for level in levels]
    whole = functools.reduce(jnp.add, parts)
    acc = sum(part * in_ref[g, :count, :] for g, part in enumerate(parts))
    out_ref[...] = (acc / whole).astype(out_ref.dtype)


def blend(me, packets, steps, share, groups, rows):
    return pl.pallas_call(
        functools.partial(blend_body, steps=steps, share=share, groups=groups, rows=rows),
        in_specs=smem(1) + vmem(1), out_specs=vmem(1)[0],
        out_shape=jax.ShapeDtypeStruct((steps * share, LANES), jnp.bfloat16),
        compiler_params=params(8),
        name="blend",
    )(me.reshape(1), packets)


def spread(pairs):
    return [(2 * a + core, 2 * b + core) for a, b in pairs for core in (0, 1)]


def shards(
    stretch_keys, stretch_values, stretch_assign, centroid_keys, centroid_values, cluster_counts,
    cache_keys, cache_values, block_cluster, selected, queries,
):
    clusters, width = centroid_keys.shape[1:]
    groups = lax.axis_size("ctx")
    me = lax.axis_index("ctx")
    owned = clusters // groups
    chips = groups // 2
    chip, core = me // 2, me % 2
    swap = [(i, i ^ 1) for i in range(groups)]

    mine = (stretch_keys[0], stretch_values[0], stretch_assign)
    other = tuple(lax.ppermute(a, "ctx", swap) for a in mine)
    counts = chip_counts(mine[2], other[2], clusters)

    def sums_for(target, dtype):
        spot = (2 * target + core).astype(jnp.int32)
        return segment_sums(spot, (mine, other), None, counts, owned, dtype)

    def move(a, pairs):
        return lax.ppermute(a, "ctx", spread(pairs))

    bf16 = jnp.bfloat16
    if chips == 4:
        left = chip < 2
        end = jnp.logical_or(chip == 0, chip == 3)
        spot = (2 * jnp.where(left, 3, 0) + core).astype(jnp.int32)
        slot0 = segment_sums(spot, (mine,), None, None, owned, jnp.float32)
        slot0 = segment_sums(spot, (other,), slot0, counts, owned, bf16)
        first = move(slot0, [(0, 1), (3, 2)])
        slot1 = sums_for(jnp.where(left, 2, 1), bf16)
        skip = move(slot1, [(0, 2), (3, 1)])
        across = move(slot1, [(1, 2), (2, 1)])
        slot2 = sums_for(jnp.where(left, jnp.where(end, 1, 0), jnp.where(end, 2, 3)), bf16)
        beside = move(slot2, [(0, 1), (1, 0), (2, 3), (3, 2)])
        passed = relay(slot0, first, owned)
        far = move(passed, [(1, 3), (2, 0)])
        came = [skip, across, beside, far]
    else:
        came = []
        for d in range(1, chips):
            slot = sums_for((chip + d) % chips, bf16)
            came.append(move(slot, [(i, (i + d) % chips) for i in range(chips)]))
    own = sums_for(chip, jnp.float32)

    heads = lax.axis_size("head")
    head = lax.axis_index("head")
    asked = list(by_head(head.astype(jnp.int32), queries))
    for d in range(1, heads):
        asked[d] = lax.ppermute(asked[d], "head", [(i, (i + d) % heads) for i in range(heads)])
    steps = queries.shape[0]
    query_rows = heads * queries.shape[1]
    *dense, query, own_bias = dense_part(
        me.astype(jnp.int32), head.astype(jnp.int32), asked, cache_keys[0], cache_values[0],
        block_cluster, *mine, selected[:, 0], owned,
    )
    new_keys, new_values, new_counts, packets = finish(
        me.astype(jnp.int32), own, came,
        lax.dynamic_slice_in_dim(centroid_keys[0], me * owned, owned, 0),
        lax.dynamic_slice_in_dim(centroid_values[0], me * owned, owned, 0),
        lax.dynamic_slice_in_dim(cluster_counts[0], me * owned, owned, 0).reshape(1, -1, LANES),
        own_bias, query, dense, groups, owned,
    )
    packets = lax.all_to_all(packets, "ctx", split_axis=0, concat_axis=0, tiled=True)
    share = query_rows // groups
    result = blend(me.astype(jnp.int32), packets, steps, share, groups, query_rows)
    return (
        new_keys[None],
        new_values[None],
        new_counts.reshape(1, owned),
        result.reshape(steps, 1, share, width),
    )


def solution(mesh):
    in_specs = (
        P("head", "ctx", None),
        P("head", "ctx", None),
        P("head", "ctx"),
        P("head", None, None),
        P("head", None, None),
        P("head", None),
        P("head", "ctx", None),
        P("head", "ctx", None),
        P("head", "ctx"),
        P(None, "head", None),
        P(None, "head", None, None),
    )
    out_specs = (
        P("head", "ctx", None),
        P("head", "ctx", None),
        P("head", "ctx"),
        P(None, "head", "ctx", None),
    )
    return jax.shard_map(shards, mesh=mesh, in_specs=in_specs, out_specs=out_specs, check_vma=False)
```

profile of v0, /device:TPU:0, one launch (start us, length us, event | category | flops | bytes accessed | tf_op | source)
XLA Modules:
  0.0 57.6 jit_solution(1410418434220739140)
XLA Ops:
  0.6 0.0 copy-start
  0.6 0.6 collective-permute-start
  1.2 0.1 collective-permute-start.1
  1.3 0.4 collective-permute-start.2
  1.7 0.8 %copy-done.11 = bf16[4,16,4,128]{3,2,1,0:T(4,128)(2,1)S(1)} copy-done((bf16[4,16,4,128]{3,2,1,0:T(4,128)(2,1)S(1)}, bf16[4,16,4,128]{3,2,1,0:T(4,128)(2,1)}, u32[]{:S(2)}) %copy-start.11) | copy-done | bytes 65560
  2.6 3.6 %collective-permute-start.10 = (bf16[64,128]{1,0:T(8,128)(2,1)S(1)}, bf16[64,128]{1,0:T(8,128)(2,1)S(1)}, u32[]{:S(2)}, u32[]{:S(2)}) collective-permute-start(bf16[64,128]{1,0:T(8,128)(2,1)S(1)} %get-tuple-element.20), channel_id=1, source_target_pairs={{0,3},{1,0},{2,1},{3,2},{4,7},{5,4},{6,5},{7,6},{8,11},{9,8},{10,9... | collective-permute-start | bytes 49160 | tf_op jit(solution)/shard_map/ppermute | solution.py:466
  6.2 0.1 pad_add_fusion.me_ref
  6.2 1.1 %dynamic-slice_bitcast_fusion = (f32[512,128]{1,0:T(8,128)S(1)}, f32[512,128]{1,0:T(8,128)S(1)}) fusion(f32[1,4096,128]{2,1,0:T(8,128)} %param.15, s32[]{:T(128)S(6)} %select_n.40, f32[1,4096,128]{2,1,0:T(8,128)} %param.14), kind=kLoop, calls=%fused_computation | loop fusion | bytes 1048580 | tf_op jit(solution)/shard_map/dynamic_slice | solution.py:476
  7.3 0.0 copy-start.3
  7.3 1.2 %copy-done.3 = bf16[1,4096,128]{2,1,0:T(8,128)(2,1)S(1)} copy-done((bf16[1,4096,128]{2,1,0:T(8,128)(2,1)S(1)}, bf16[1,4096,128]{2,1,0:T(8,128)(2,1)}, u32[]{:S(2)}) %copy-start.3) | copy-done | bytes 1048600
  8.5 1.2 %copy-done.5 = bf16[1,4096,128]{2,1,0:T(8,128)(2,1)S(1)} copy-done((bf16[1,4096,128]{2,1,0:T(8,128)(2,1)S(1)}, bf16[1,4096,128]{2,1,0:T(8,128)(2,1)}, u32[]{:S(2)}) %copy-start.5) | copy-done | bytes 1048600
  9.8 0.7 %copy-done.7 = s32[1,4096]{1,0:T(1,128)S(1)} copy-done((s32[1,4096]{1,0:T(1,128)S(1)}, s32[1,4096]{1,0:T(1,128)}, u32[]{:S(2)}) %copy-start.7) | copy-done | bytes 16408
  10.5 1.2 %shard_map.141.refs_3_ = f32[512,256]{1,0:T(8,128)S(1)} custom-call(s32[1]{0:T(128)} %bitcast.7.slot_ref, bf16[4096,128]{1,0:T(8,128)(2,1)S(1)} %bitcast.27, bf16[4096,128]{1,0:T(8,128)(2,1)S(1)} %bitcast.33, s32[1,4096]{1,0:T(1,128)S(1)} %copy-done.7), custom_call_target="tpu_custom_call" | custom-call | flops 1073741824 | bytes 1048576 | tf_op jit(solution)/shard_map/pallas_call | solution.py:123
  11.8 1.2 %collective-permute-start.9 = (bf16[64,128]{1,0:T(8,128)(2,1)S(1)}, bf16[64,128]{1,0:T(8,128)(2,1)S(1)}, u32[]{:S(2)}, u32[]{:S(2)}) collective-permute-start(bf16[64,128]{1,0:T(8,128)(2,1)S(1)} %get-tuple-element.19), channel_id=1, source_target_pairs={{0,2},{1,3},{2,0},{3,1},{4,6},{5,7},{6,4},{7,5},{8,10},{9,11},{10,... | collective-permute-start | bytes 49160 | tf_op jit(solution)/shard_map/ppermute | solution.py:466
  12.9 0.8 %chip_counts.1 = f32[32,128]{1,0:T(8,128)S(1)} custom-call(s32[1,4096]{1,0:T(1,128)S(1)} %copy-done.8, s32[1,4096]{1,0:T(1,128)S(1)} %collective-permute-done.2.other_ref.refs_5_.refs_2_), custom_call_target="tpu_custom_call" | custom-call | flops 1000000000 | bytes 1048576 | tf_op jit(solution)/shard_map/chip_counts/pallas_call | solution.py:73
  13.7 0.0 copy-start.6
  13.8 1.3 %shard_map.142.own_ref = bf16[528,256]{1,0:T(8,128)(2,1)S(1)} custom-call(s32[1]{0:T(128)} %bitcast.7.slot_ref, bf16[4096,128]{1,0:T(8,128)(2,1)S(1)} %collective-permute-done.refs_3_.refs_0_, bf16[4096,128]{1,0:T(8,128)(2,1)S(1)} %collective-permute-done.1.refs_4_.refs_1_, s32[1,4096]{1,0:T(1,128)S(1)} %collective-permute-done.2.other_ref.refs_5_.refs_2_, ...), custom_call_target="tpu_custom_call" | custom-call | flops 1073741824 | bytes 1048576 | tf_op jit(solution)/shard_map/pallas_call | solution.py:123
  15.0 3.5 %collective-permute-start.6 = (bf16[528,256]{1,0:T(8,128)(2,1)S(1)}, bf16[528,256]{1,0:T(8,128)(2,1)S(1)}, u32[]{:S(2)}, u32[]{:S(2)}) collective-permute-start(bf16[528,256]{1,0:T(8,128)(2,1)S(1)} %shard_map.142.own_ref), channel_id=1, source_target_pairs={{0,8},{4,12},{24,16},{28,20},{1,9},{5,13},{25,17},{29,21},{2,10},{... | collective-permute-start | bytes 811016 | tf_op jit(solution)/shard_map/ppermute | solution.py:437
  18.6 2.3 %shard_map.139 = bf16[528,256]{1,0:T(8,128)(2,1)S(1)} custom-call(s32[1]{0:T(128)} %bitcast.5.slot_ref, bf16[4096,128]{1,0:T(8,128)(2,1)S(1)} %bitcast.28, bf16[4096,128]{1,0:T(8,128)(2,1)S(1)} %bitcast.34, s32[1,4096]{1,0:T(1,128)S(1)} %copy-done.8, bf16[4096,128]{1,0:T(8,128)(2,1)S(1)} %collective-permute-done.refs_3_.refs_0_, ...), custom_call_target="tpu_custom_call" | custom-call | flops 2147483648 | bytes 1048576 | tf_op jit(solution)/shard_map/pallas_call | solution.py:123
  20.9 2.3 %collective-permute-start.3 = (bf16[528,256]{1,0:T(8,128)(2,1)S(1)}, bf16[528,256]{1,0:T(8,128)(2,1)S(1)}, u32[]{:S(2)}, u32[]{:S(2)}) collective-permute-start(bf16[528,256]{1,0:T(8,128)(2,1)S(1)} %shard_map.139), channel_id=1, source_target_pairs={{0,16},{4,20},{24,8},{28,12},{1,17},{5,21},{25,9},{29,13},{2,18},{... | collective-permute-start | bytes 811016 | tf_op jit(solution)/shard_map/ppermute | solution.py:437
  23.2 2.3 %shard_map.140 = bf16[528,256]{1,0:T(8,128)(2,1)S(1)} custom-call(s32[1]{0:T(128)} %bitcast.6.slot_ref, bf16[4096,128]{1,0:T(8,128)(2,1)S(1)} %bitcast.29, bf16[4096,128]{1,0:T(8,128)(2,1)S(1)} %bitcast.35, s32[1,4096]{1,0:T(1,128)S(1)} %copy-done.8, bf16[4096,128]{1,0:T(8,128)(2,1)S(1)} %collective-permute-done.refs_3_.refs_0_, ...), custom_call_target="tpu_custom_call" | custom-call | flops 2147483648 | bytes 1048576 | tf_op jit(solution)/shard_map/pallas_call | solution.py:123
  25.6 0.0 copy-start.9
  25.6 0.8 %collective-permute-start.4 = (bf16[528,256]{1,0:T(8,128)(2,1)S(1)}, bf16[528,256]{1,0:T(8,128)(2,1)S(1)}, u32[]{:S(2)}, u32[]{:S(2)}) collective-permute-start(bf16[528,256]{1,0:T(8,128)(2,1)S(1)} %shard_map.139), channel_id=1, source_target_pairs={{8,16},{12,20},{16,8},{20,12},{9,17},{13,21},{17,9},{21,13},{10,18... | collective-permute-start | bytes 811016 | tf_op jit(solution)/shard_map/ppermute | solution.py:437
  26.4 0.1 relay.1
  26.5 5.0 %collective-permute-start.5 = (bf16[528,256]{1,0:T(8,128)(2,1)S(1)}, bf16[528,256]{1,0:T(8,128)(2,1)S(1)}, u32[]{:S(2)}, u32[]{:S(2)}) collective-permute-start(bf16[528,256]{1,0:T(8,128)(2,1)S(1)} %shard_map.140), channel_id=1, source_target_pairs={{0,8},{4,12},{8,0},{12,4},{16,24},{20,28},{24,16},{28,20},{1,9},{5... | collective-permute-start | bytes 811016 | tf_op jit(solution)/shard_map/ppermute | solution.py:437
  31.5 1.3 %collective-permute-start.7 = (bf16[528,256]{1,0:T(8,128)(2,1)S(1)}, bf16[528,256]{1,0:T(8,128)(2,1)S(1)}, u32[]{:S(2)}, u32[]{:S(2)}) collective-permute-start(bf16[528,256]{1,0:T(8,128)(2,1)S(1)} %relay.1), channel_id=1, source_target_pairs={{8,24},{12,28},{16,0},{20,4},{9,25},{13,29},{17,1},{21,5},{10,26},... | collective-permute-start | bytes 811016 | tf_op jit(solution)/shard_map/ppermute | solution.py:437
  32.8 7.8 %dense_part.1 = (f32[256,1]{1,0:T(8,128)S(1)}, f32[256,1]{1,0:T(8,128)S(1)}, f32[256,128]{1,0:T(8,128)S(1)}, f32[256,128]{1,0:T(8,128)S(1)}, f32[4,512]{1,0:T(4,128)S(1)}) custom-call(s32[2]{0:T(128)S(1)} %pad_add_fusion.me_ref, bf16[64,128]{1,0:T(8,128)(2,1)S(1)} %get-tuple-element.17.refs_0_, bf16[64,128]{1,0:T(8,128)(2,1)S(1)} %collective-permute-done.8.refs_1_, ...), custom_call_target="tpu_custom_call" | custom-call | flops 1610612736 | bytes 1048576 | tf_op jit(solution)/shard_map/dense_part/pallas_call | solution.py:271
  40.6 2.3 %shard_map.138.own_ref = f32[528,256]{1,0:T(8,128)S(1)} custom-call(s32[1]{0:T(128)} %bitcast.1.slot_ref, bf16[4096,128]{1,0:T(8,128)(2,1)S(1)} %bitcast.31, bf16[4096,128]{1,0:T(8,128)(2,1)S(1)} %bitcast.37, s32[1,4096]{1,0:T(1,128)S(1)} %copy-done.8, bf16[4096,128]{1,0:T(8,128)(2,1)S(1)} %collective-permute-done.refs_3_.refs_0_, ...), custom_call_target="tpu_custom_call" | custom-call | flops 2147483648 | bytes 1048576 | tf_op jit(solution)/shard_map/pallas_call | solution.py:123
  43.0 1.3 %collective-permute-done.7.refs_3_ = bf16[528,256]{1,0:T(8,128)(2,1)S(1)} collective-permute-done((bf16[528,256]{1,0:T(8,128)(2,1)S(1)}, bf16[528,256]{1,0:T(8,128)(2,1)S(1)}, u32[]{:S(2)}, u32[]{:S(2)}) %collective-permute-start.7) | collective-permute-done | bytes 270368 | tf_op jit(solution)/shard_map/ppermute | solution.py:437
  44.3 2.1 %finish.1 = (f32[512,128]{1,0:T(8,128)}, f32[512,128]{1,0:T(8,128)}, f32[1,4,128]{2,1,0:T(4,128)}, f32[8,40,128]{2,1,0:T(8,128)S(1)}) custom-call(s32[1]{0:T(128)} %bitcast.me_ref, f32[528,256]{1,0:T(8,128)S(1)} %shard_map.138.own_ref, bf16[528,256]{1,0:T(8,128)(2,1)S(1)} %collective-permute-done.3.refs_0_, ...), custom_call_target="tpu_custom_call" | custom-call | flops 4000000000 | bytes 1048576 | tf_op jit(solution)/shard_map/finish/pallas_call | solution.py:364
  46.4 10.5 %all_to_all.5.in_ref = f32[8,40,128]{2,1,0:T(8,128)S(1)} all-to-all(f32[8,40,128]{2,1,0:T(8,128)S(1)} %get-tuple-element.29), channel_id=1, replica_groups=mesh['ctx'=8,'head'=4] {'ctx'}, dimensions={0} | all-to-all | bytes 327680 | tf_op jit(solution)/shard_map/all_to_all | solution.py:480
  56.8 0.7 %blend.1 = bf16[32,128]{1,0:T(8,128)(2,1)} custom-call(s32[1]{0:T(128)} %bitcast.me_ref, f32[8,40,128]{2,1,0:T(8,128)S(1)} %all_to_all.5.in_ref), custom_call_target="tpu_custom_call" | custom-call | tf_op jit(solution)/shard_map/blend/pallas_call | solution.py:403
  (29 shorter events, 0.1 us)
Async XLA Ops:
  0.6 5.6 %copy-start = (f32[1,4096]{1,0:T(1,128)S(1)}, f32[1,4096]{1,0:T(1,128)}, u32[]{:S(2)}) copy-start(f32[1,4096]{1,0:T(1,128)} %param.16) | copy-start | bytes 49156
  0.6 13.1 %collective-permute-start = (bf16[4096,128]{1,0:T(8,128)(2,1)}, bf16[4096,128]{1,0:T(8,128)(2,1)S(1)}, u32[]{:S(2)}, u32[]{:S(2)}) collective-permute-start(bf16[4096,128]{1,0:T(8,128)(2,1)} %bitcast.26), channel_id=1, source_target_pairs={{0,4},{4,0},{8,12},{12,8},{16,20},{20,16},{24,28},{28,24},{1,5},{5... | collective-permute-start | bytes 3145736 | tf_op jit(solution)/shard_map/ppermute | solution.py:429
  1.2 12.6 %collective-permute-start.1 = (bf16[4096,128]{1,0:T(8,128)(2,1)}, bf16[4096,128]{1,0:T(8,128)(2,1)S(1)}, u32[]{:S(2)}, u32[]{:S(2)}) collective-permute-start(bf16[4096,128]{1,0:T(8,128)(2,1)} %bitcast.32), channel_id=1, source_target_pairs={{0,4},{4,0},{8,12},{12,8},{16,20},{20,16},{24,28},{28,24},{1,5},{5... | collective-permute-start | bytes 3145736 | tf_op jit(solution)/shard_map/ppermute | solution.py:429
  1.3 10.5 %collective-permute-start.2 = (s32[1,4096]{1,0:T(1,128)}, s32[1,4096]{1,0:T(1,128)S(1)}, u32[]{:S(2)}, u32[]{:S(2)}) collective-permute-start(s32[1,4096]{1,0:T(1,128)} %refs_9_.1), channel_id=1, source_target_pairs={{0,4},{4,0},{8,12},{12,8},{16,20},{20,16},{24,28},{28,24},{1,5},{5... | collective-permute-start | bytes 49160 | tf_op jit(solution)/shard_map/ppermute | solution.py:429
  1.7 0.8 %copy-start.11 = (bf16[4,16,4,128]{3,2,1,0:T(4,128)(2,1)S(1)}, bf16[4,16,4,128]{3,2,1,0:T(4,128)(2,1)}, u32[]{:S(2)}) copy-start(bf16[4,16,4,128]{3,2,1,0:T(4,128)(2,1)} %param.21) | copy-start | bytes 196612
  2.6 23.9 %collective-permute-start.10 = (bf16[64,128]{1,0:T(8,128)(2,1)S(1)}, bf16[64,128]{1,0:T(8,128)(2,1)S(1)}, u32[]{:S(2)}, u32[]{:S(2)}) collective-permute-start(bf16[64,128]{1,0:T(8,128)(2,1)S(1)} %get-tuple-element.20), channel_id=1, source_target_pairs={{0,3},{1,0},{2,1},{3,2},{4,7},{5,4},{6,5},{7,6},{8,11},{9,8},{10,9... | collective-permute-start | bytes 49160 | tf_op jit(solution)/shard_map/ppermute | solution.py:466
  6.2 25.3 %collective-permute-start.8 = (bf16[64,128]{1,0:T(8,128)(2,1)S(1)}, bf16[64,128]{1,0:T(8,128)(2,1)S(1)}, u32[]{:S(2)}, u32[]{:S(2)}) collective-permute-start(bf16[64,128]{1,0:T(8,128)(2,1)S(1)} %get-tuple-element.18), channel_id=1, source_target_pairs={{0,1},{1,2},{2,3},{3,0},{4,5},{5,6},{6,7},{7,4},{8,9},{9,10},{10,1... | collective-permute-start | bytes 49160 | tf_op jit(solution)/shard_map/ppermute | solution.py:466
  7.3 1.2 %copy-start.3 = (bf16[1,4096,128]{2,1,0:T(8,128)(2,1)S(1)}, bf16[1,4096,128]{2,1,0:T(8,128)(2,1)}, u32[]{:S(2)}) copy-start(bf16[1,4096,128]{2,1,0:T(8,128)(2,1)} %param.11) | copy-start | bytes 3145732
  8.5 1.2 %copy-start.5 = (bf16[1,4096,128]{2,1,0:T(8,128)(2,1)S(1)}, bf16[1,4096,128]{2,1,0:T(8,128)(2,1)}, u32[]{:S(2)}) copy-start(bf16[1,4096,128]{2,1,0:T(8,128)(2,1)} %param.12) | copy-start | bytes 3145732
  9.8 0.7 %copy-start.7 = (s32[1,4096]{1,0:T(1,128)S(1)}, s32[1,4096]{1,0:T(1,128)}, u32[]{:S(2)}) copy-start(s32[1,4096]{1,0:T(1,128)} %refs_9_.1) | copy-start | bytes 49156
  10.5 2.5 %copy-start.8 = (s32[1,4096]{1,0:T(1,128)S(1)}, s32[1,4096]{1,0:T(1,128)}, u32[]{:S(2)}) copy-start(s32[1,4096]{1,0:T(1,128)} %refs_9_.1) | copy-start | bytes 49156
  11.8 21.0 %collective-permute-start.9 = (bf16[64,128]{1,0:T(8,128)(2,1)S(1)}, bf16[64,128]{1,0:T(8,128)(2,1)S(1)}, u32[]{:S(2)}, u32[]{:S(2)}) collective-permute-start(bf16[64,128]{1,0:T(8,128)(2,1)S(1)} %get-tuple-element.19), channel_id=1, source_target_pairs={{0,2},{1,3},{2,0},{3,1},{4,6},{5,7},{6,4},{7,5},{8,10},{9,11},{10,... | collective-permute-start | bytes 49160 | tf_op jit(solution)/shard_map/ppermute | solution.py:466
  13.7 4.8 %copy-start.4 = (bf16[1,4096,128]{2,1,0:T(8,128)(2,1)S(1)}, bf16[1,4096,128]{2,1,0:T(8,128)(2,1)}, u32[]{:S(2)}) copy-start(bf16[1,4096,128]{2,1,0:T(8,128)(2,1)} %param.11) | copy-start | bytes 3145732
  13.7 4.8 %copy-start.6 = (bf16[1,4096,128]{2,1,0:T(8,128)(2,1)S(1)}, bf16[1,4096,128]{2,1,0:T(8,128)(2,1)}, u32[]{:S(2)}) copy-start(bf16[1,4096,128]{2,1,0:T(8,128)(2,1)} %param.12) | copy-start | bytes 3145732
  15.0 10.6 %collective-permute-start.6 = (bf16[528,256]{1,0:T(8,128)(2,1)S(1)}, bf16[528,256]{1,0:T(8,128)(2,1)S(1)}, u32[]{:S(2)}, u32[]{:S(2)}) collective-permute-start(bf16[528,256]{1,0:T(8,128)(2,1)S(1)} %shard_map.142.own_ref), channel_id=1, source_target_pairs={{0,8},{4,12},{24,16},{28,20},{1,9},{5,13},{25,17},{29,21},{2,10},{... | collective-permute-start | bytes 811016 | tf_op jit(solution)/shard_map/ppermute | solution.py:437
  20.9 22.0 %collective-permute-start.3 = (bf16[528,256]{1,0:T(8,128)(2,1)S(1)}, bf16[528,256]{1,0:T(8,128)(2,1)S(1)}, u32[]{:S(2)}, u32[]{:S(2)}) collective-permute-start(bf16[528,256]{1,0:T(8,128)(2,1)S(1)} %shard_map.139), channel_id=1, source_target_pairs={{0,16},{4,20},{24,8},{28,12},{1,17},{5,21},{25,9},{29,13},{2,18},{... | collective-permute-start | bytes 811016 | tf_op jit(solution)/shard_map/ppermute | solution.py:437
  23.2 9.6 %copy-start.2 = (bf16[1,8192,128]{2,1,0:T(8,128)(2,1)S(1)}, bf16[1,8192,128]{2,1,0:T(8,128)(2,1)}, u32[]{:S(2)}) copy-start(bf16[1,8192,128]{2,1,0:T(8,128)(2,1)} %param.18) | copy-start | bytes 6291460
  25.6 7.2 %copy-start.1 = (bf16[1,8192,128]{2,1,0:T(8,128)(2,1)S(1)}, bf16[1,8192,128]{2,1,0:T(8,128)(2,1)}, u32[]{:S(2)}) copy-start(bf16[1,8192,128]{2,1,0:T(8,128)(2,1)} %param.17) | copy-start | bytes 6291460
  25.6 7.2 %copy-start.9 = (s32[1,512]{1,0:T(1,128)S(1)}, s32[1,512]{1,0:T(1,128)}, u32[]{:S(2)}) copy-start(s32[1,512]{1,0:T(1,128)} %refs_6_.1) | copy-start | bytes 6148
  25.6 7.2 %copy-start.10 = (s32[4,1,64]{2,1,0:T(1,128)S(1)}, s32[4,1,64]{2,1,0:T(1,128)}, u32[]{:S(2)}) copy-start(s32[4,1,64]{2,1,0:T(1,128)} %param.20) | copy-start | bytes 3076
  25.6 17.3 %collective-permute-start.4 = (bf16[528,256]{1,0:T(8,128)(2,1)S(1)}, bf16[528,256]{1,0:T(8,128)(2,1)S(1)}, u32[]{:S(2)}, u32[]{:S(2)}) collective-permute-start(bf16[528,256]{1,0:T(8,128)(2,1)S(1)} %shard_map.139), channel_id=1, source_target_pairs={{8,16},{12,20},{16,8},{20,12},{9,17},{13,21},{17,9},{21,13},{10,18... | collective-permute-start | bytes 811016 | tf_op jit(solution)/shard_map/ppermute | solution.py:437
  26.5 16.4 %collective-permute-start.5 = (bf16[528,256]{1,0:T(8,128)(2,1)S(1)}, bf16[528,256]{1,0:T(8,128)(2,1)S(1)}, u32[]{:S(2)}, u32[]{:S(2)}) collective-permute-start(bf16[528,256]{1,0:T(8,128)(2,1)S(1)} %shard_map.140), channel_id=1, source_target_pairs={{0,8},{4,12},{8,0},{12,4},{16,24},{20,28},{24,16},{28,20},{1,9},{5... | collective-permute-start | bytes 811016 | tf_op jit(solution)/shard_map/ppermute | solution.py:437
  31.5 12.8 %collective-permute-start.7 = (bf16[528,256]{1,0:T(8,128)(2,1)S(1)}, bf16[528,256]{1,0:T(8,128)(2,1)S(1)}, u32[]{:S(2)}, u32[]{:S(2)}) collective-permute-start(bf16[528,256]{1,0:T(8,128)(2,1)S(1)} %relay.1), channel_id=1, source_target_pairs={{8,24},{12,28},{16,0},{20,4},{9,25},{13,29},{17,1},{21,5},{10,26},... | collective-permute-start | bytes 811016 | tf_op jit(solution)/shard_map/ppermute | solution.py:437
where the time goes:
time: 58 us; the launch traced here: 57.6 us
  Pallas kernels  20.9 us (36%)
  starting transfers between devices  18.7 us (32%)
  blocking collectives  10.5 us (18%)
  local copies, waits for them, and re-layouts  5.14 us (9%)
  waiting for transfers between devices  1.37 us (2%)
  between operations  0.93 us (2%)
    ppermute x5, starting transfers between devices, move(): return lax.ppermute(a, 'ctx', spread(pairs))  12.9 us
    all_to_all x1, blocking collectives, shards(): lax.all_to_all(packets, 'ctx', split_axis=0, concat_axis=0, tiled=True)  10.5 us
    pallas_call x5, Pallas kernels, segment_sums(): pl.pallas_call(functools.partial(segment_body, owned=owned, sources=len(s...  9.49 us
    pallas_call x1, Pallas kernels, dense_part(): pl.pallas_call(functools.partial(dense_body, scale=width ** (-0.5) * LOG2...  7.75 us
    ppermute x3, starting transfers between devices, shards(): lax.ppermute(asked[d], 'head', [(i, (i + d) % heads) for i in range(heads)])  4.73 us
    unnamed x24, local copies, waits for them, and re-layouts  4.07 us
    pallas_call x1, Pallas kernels, finish(): pl.pallas_call(functools.partial(finish_body, owned=owned, lines=lines, s...  2.07 us
    ppermute x5, waiting for transfers between devices, move(): return lax.ppermute(a, 'ctx', spread(pairs))  1.35 us
  transfers between devices with their start and end apart: 11, of which 1 were waited for; matrix products, arithmetic and copies ran while one was open for 2% of the time, Pallas kernels for 31%

commit v1 on v0

v1 whole, which is shorter than its diff:
```python
import functools
import math
import jax
import jax.numpy as jnp
from jax import lax
from jax.experimental import pallas as pl
from jax.experimental.pallas import tpu as pltpu
from jax.sharding import PartitionSpec as P


LANES = 128
TAIL = 16
NEG = -1e30
LOG2E = math.log2(math.e)


def vmem(count):
    return [pl.BlockSpec(memory_space=pltpu.VMEM)] * count


def hbm(count):
    return [pl.BlockSpec(memory_space=pltpu.HBM)] * count


def smem(count):
    return [pl.BlockSpec(memory_space=pltpu.SMEM)] * count


def params(mib):
    return pltpu.CompilerParams(vmem_limit_bytes=mib * 2**20)


def cost(flops, moved=2**20):
    return pl.CostEstimate(flops=int(flops), bytes_accessed=int(moved), transcendentals=0)


def turn_body(head_ref, in_ref, *refs):
    outs, held = refs[:-1], refs[-1]
    heads = len(outs)
    held[...] = in_ref[...].astype(jnp.float32)
    for d, out_ref in enumerate(outs):
        head = lax.rem(head_ref[0] + d, heads)
        out_ref[...] = held[pl.ds(head, out_ref.shape[0], stride=heads), :].astype(out_ref.dtype)


def by_head(spot, queries):
    steps, rows, heads, width = queries.shape
    return pl.pallas_call(
        turn_body,
        in_specs=smem(1) + vmem(1), out_specs=vmem(heads),
        out_shape=[jax.ShapeDtypeStruct((steps * rows, width), queries.dtype)] * heads,
        scratch_shapes=[pltpu.VMEM((steps * rows * heads, width), jnp.float32)],
        compiler_params=params(4), cost_estimate=cost(1e8),
        name="by_head",
    )(spot[1], queries.reshape(steps * rows * heads, width))


def count_body(mine_ref, other_ref, out_ref, *, rows):
    total = jnp.zeros((rows, LANES), jnp.float32)
    for ref in (mine_ref, other_ref):
        ids = ref[...]
        span = ids.shape[1]
        upper = (ids // LANES).astype(jnp.int16)
        lower = (ids % LANES).astype(jnp.int16)
        high = lax.broadcasted_iota(jnp.int16, (rows, span), 0) == upper
        low = lax.broadcasted_iota(jnp.int16, (LANES, span), 0) == lower
        one, none = jnp.bfloat16(1), jnp.bfloat16(0)
        total = total + lax.dot_general(
            jnp.where(high, one, none), jnp.where(low, one, none),
            (((1,), (1,)), ((), ())), preferred_element_type=jnp.float32,
        )
    out_ref[...] = total


def chip_counts(mine, other, clusters):
    rows = clusters // LANES
    return pl.pallas_call(
        functools.partial(count_body, rows=rows),
        in_specs=vmem(2), out_specs=vmem(1)[0],
        out_shape=jax.ShapeDtypeStruct((rows, LANES), jnp.float32),
        compiler_params=params(8), cost_estimate=cost(1e9),
        name="chip_counts",
    )(mine, other)


def slot_of(spot_ref, turn, chips):
    chip, core = spot_ref[0] // 2, spot_ref[0] % 2
    target = chip ^ turn if chips == 4 else lax.rem(chip + turn, chips)
    return 2 * target + core


def segment_body(spot_ref, head_ref, *refs, owned, sources, started, counted, turn, chips):
    out_ref = refs[-1]
    slot = slot_of(spot_ref, turn, chips)
    base = slot * owned
    parts = [refs[3 * sources][...]] if started else []
    positions = refs[0].shape[0]
    span = min(2048, positions)
    for i in range(sources):
        keys, values, ids = refs[3 * i : 3 * i + 3]
        for at in range(0, positions, span):
            near = (ids[:, at : at + span] - base).astype(jnp.int16)
            spots = lax.broadcasted_iota(jnp.int16, (owned, span), 0)
            hot = jnp.where(spots == near, jnp.bfloat16(1), jnp.bfloat16(0))
            rows = jnp.concatenate([keys[at : at + span, :], values[at : at + span, :]], axis=1)
            parts.append(jnp.dot(hot, rows, preferred_element_type=jnp.float32))
    total = functools.reduce(jnp.add, parts)
    if not counted:
        out_ref[...] = total
        return
    out_ref[:owned, :] = total.astype(out_ref.dtype)
    counts = refs[3 * sources + started][slot]
    high = jnp.floor(counts * (1.0 / 256.0))
    low = counts - 256.0 * high
    lines = counts.shape[0]
    packed = jnp.concatenate([high, low], axis=1)
    packed = jnp.concatenate(
        [packed, jnp.zeros((TAIL - lines, 2 * LANES), jnp.float32)], axis=0
    )
    out_ref[owned:, :] = packed.astype(out_ref.dtype)


def segment_sums(spot, turn, chips, sources, start, counts, owned, dtype):
    positions, width = sources[0][0].shape
    lines = owned // LANES
    args = [*spot]
    for source in sources:
        args += source
    if start is not None:
        args.append(start)
    if counts is not None:
        args.append(counts.reshape(-1, lines, LANES))
    height = owned if counts is None else owned + TAIL
    return pl.pallas_call(
        functools.partial(
            segment_body, owned=owned, sources=len(sources), started=start is not None,
            counted=counts is not None, turn=turn, chips=chips,
        ),
        in_specs=smem(2) + vmem(len(args) - 2), out_specs=vmem(1)[0],
        out_shape=jax.ShapeDtypeStruct((height, 2 * width), dtype),
        compiler_params=params(12),
        cost_estimate=cost(4 * len(sources) * positions * owned * width),
    )(*args)


def home_body(spot_ref, ck_hbm, cv_hbm, *refs, owned, **sizes):
    sources = refs[:7]
    out_ref, ck, cv, sems = refs[7:]
    rows = pl.ds(pl.multiple_of(spot_ref[0] * owned, owned), owned)
    copies = [
        pltpu.make_async_copy(src.at[rows, :], dst, sems.at[i])
        for i, (src, dst) in enumerate(((ck_hbm, ck), (cv_hbm, cv)))
    ]
    for copy in copies:
        copy.start()
    segment_body(
        spot_ref, None, *sources, out_ref, owned=owned, sources=2, started=False, counted=True, **sizes
    )
    for copy in copies:
        copy.wait()


def home_sums(spot, chips, mine, other, counts, cent_k, cent_v, owned):
    positions, width = mine[0].shape
    f32 = jnp.float32
    lines = owned // LANES
    return pl.pallas_call(
        functools.partial(home_body, owned=owned, turn=0, chips=chips),
        in_specs=smem(1) + hbm(2) + vmem(7), out_specs=vmem(3),
        out_shape=[
            jax.ShapeDtypeStruct((owned + TAIL, 2 * width), f32),
            jax.ShapeDtypeStruct((owned, width), f32),
            jax.ShapeDtypeStruct((owned, width), f32),
        ],
        scratch_shapes=[pltpu.SemaphoreType.DMA((2,))],
        compiler_params=params(12), cost_estimate=cost(8 * positions * owned * width),
        name="home_sums",
    )(spot[0], cent_k, cent_v, *mine, *other, counts.reshape(-1, lines, LANES))


def relay_body(own_ref, came_ref, out_ref, *, owned, lines):
    out_ref[:owned, :] = (
        own_ref[:owned, :].astype(jnp.float32) + came_ref[:owned, :].astype(jnp.float32)
    ).astype(out_ref.dtype)
    tail_own = own_ref[owned:, :].astype(jnp.float32)
    tail_came = came_ref[owned:, :].astype(jnp.float32)
    out_ref[owned:, :] = jnp.concatenate(
        [tail_own[:lines], tail_came[:lines], tail_own[2 * lines :]], axis=0
    ).astype(out_ref.dtype)


def relay(own, came, owned):
    return pl.pallas_call(
        functools.partial(relay_body, owned=owned, lines=owned // LANES),
        in_specs=vmem(2), out_specs=vmem(1)[0],
        out_shape=jax.ShapeDtypeStruct(own.shape, own.dtype),
        compiler_params=params(8), cost_estimate=cost(1e9),
        name="relay",
    )(own, came)


def dense_body(
    spot_ref, head_ref, *refs, scale, steps, span, block_len, heads
):
    asked = refs[:heads]
    (kc, vc, blocks, ks, vs, ids, sel_ref,
    peak_ref, whole_ref, acc_ref, q_ref, own_ref, query, held, best, sums, cache_bias, cache_hit, near_bias, light,
    kept_k, kept_v, list_v, list_s, sem) = refs[heads:]
    rows = q_ref.shape[0] // steps
    piece = rows // heads
    for d, ref in enumerate(asked):
        part = ref[...].astype(jnp.float32)
        source = lax.rem(head_ref[0] + heads - d, heads)
        for s in range(steps):
            at = pl.ds(pl.multiple_of(s * rows + source * piece, piece), piece)
            q_ref[at, :] = part[s * piece : (s + 1) * piece]
    query[...] = q_ref[...].astype(query.dtype)
    chosen = sel_ref.shape[1]
    eye = lax.broadcasted_iota(jnp.int32, (chosen, chosen), 0) == lax.broadcasted_iota(
        jnp.int32, (chosen, chosen), 1
    )
    wanted = jnp.concatenate(
        [
            jnp.broadcast_to(
                jnp.sum(
                    jnp.where(eye, sel_ref[s : s + 1, :].astype(jnp.float32), 0.0),
                    axis=1, keepdims=True,
                ),
                (chosen, LANES),
            )
            for s in range(steps)
        ],
        axis=0,
    )
    wanted = wanted.astype(jnp.int32).astype(jnp.int16)
    tell = jnp.where(
        lax.broadcasted_iota(jnp.int32, (8, steps * chosen), 0)
        == lax.broadcasted_iota(jnp.int32, (8, steps * chosen), 1) // chosen,
        1.0, 0.0,
    ).astype(jnp.bfloat16)

    def missing(names):
        names = names.astype(jnp.int16)
        same = jnp.concatenate(
            [
                jnp.where(
                    wanted == names[:, i : i + LANES], jnp.bfloat16(1), jnp.bfloat16(0)
                )
                for i in range(0, names.shape[1], LANES)
            ],
            axis=1,
        )
        found = jnp.dot(tell, same, preferred_element_type=jnp.float32)
        return jnp.where(found[:steps] > 0.5, 0.0, 1.0)

    owned = own_ref.shape[1]
    mine = spot_ref[0] * owned + lax.broadcasted_iota(jnp.int32, (1, owned), 1)
    own_ref[...] = (1.0 - missing(mine)) * NEG
    found = 1.0 - missing(blocks[...])
    count = found.shape[1]
    live = jnp.max(found, axis=0, keepdims=True)
    down = lax.broadcasted_iota(jnp.int32, (count, count), 0)
    along = lax.broadcasted_iota(jnp.int32, (count, count), 1)
    one, none = jnp.bfloat16(1), jnp.bfloat16(0)
    ahead = jnp.dot(
        jnp.broadcast_to(live, (8, count)).astype(jnp.bfloat16),
        jnp.where((down < along).astype(jnp.int16) > 0, one, none),
        preferred_element_type=jnp.float32,
    )[:1]
    place = jnp.where(live > 0.5, ahead, -1.0).astype(jnp.int32)
    chart = jnp.where((place == down).astype(jnp.int16) > 0, one, none)
    names = lax.broadcasted_iota(jnp.int32, (1, count), 1)
    table = jnp.concatenate(
        [(names // 64).astype(jnp.float32), (names % 64).astype(jnp.float32), found]
        + [jnp.zeros((6 - steps, count), jnp.float32)],
        axis=0,
    )
    packed = lax.dot_general(
        table.astype(jnp.bfloat16), chart, (((1,), (1,)), ((), ())),
        preferred_element_type=jnp.float32,
    )
    cache_hit[...] = packed[2 : 2 + steps]
    total = jnp.broadcast_to(jnp.sum(live, axis=1, keepdims=True), (1, count))
    list_v[...] = jnp.concatenate([64.0 * packed[:1] + packed[1:2], total], axis=0).astype(jnp.int32)
    listing = pltpu.make_async_copy(list_v, list_s, sem)
    listing.start()
    for at in range(0, ids.shape[1], 1024):
        near_bias[:, at : at + 1024] = missing(ids[:, at : at + 1024]) * NEG

    per = span // block_len
    widen = jnp.where(
        lax.broadcasted_iota(jnp.int32, (per, span), 0)
        == lax.broadcasted_iota(jnp.int32, (per, span), 1) // block_len,
        1.0, 0.0,
    ).astype(jnp.bfloat16)
    best[...] = jnp.full_like(best, NEG)
    sums[...] = jnp.zeros_like(sums)
    acc_ref[...] = jnp.zeros_like(acc_ref)

    def score(keys, at, shift, base):
        size = at.size
        found = lax.dot_general(
            query[...], keys[at, :], (((1,), (1,)), ((), ())), preferred_element_type=jnp.float32
        )
        found = found * scale
        found = jnp.concatenate(
            [found[s * rows : (s + 1) * rows] + shift[s : s + 1] for s in range(steps)], axis=0
        )
        held[:, pl.ds(pl.multiple_of(base + at.start, size), size)] = found
        top = best[...]
        for i in range(size // LANES):
            top = jnp.maximum(top, found[:, i * LANES : (i + 1) * LANES])
        best[...] = top

    def window(turn, span=span):
        return pl.ds(pl.multiple_of(turn * span, span), span)

    def score_near(turn, carry):
        score(ks, window(turn), near_bias[:, window(turn)], 0)
        return carry

    near = ks.shape[0]
    lax.fori_loop(0, near // span, score_near, 0)
    listing.wait()
    lively = list_s[1, 0]
    part = min(512, span)
    turns = (lively * block_len + part - 1) // part

    @pl.when(turns > 0)
    def _():
        last = window(turns - 1, part)
        kept_k[last, :] = jnp.zeros((part, kept_k.shape[1]), kept_k.dtype)
        kept_v[last, :] = jnp.zeros((part, kept_v.shape[1]), kept_v.dtype)

    def keep(n, carry):
        source = window(list_s[0, n], block_len)
        target = window(n, block_len)
        kept_k[target, :] = kc[source, :]
        kept_v[target, :] = vc[source, :]
        return carry

    lax.fori_loop(0, lively, keep, 0)

    def shift_cache(turn, carry):
        hit = cache_hit[:, pl.ds(pl.multiple_of(turn * per, per), per)].astype(jnp.bfloat16)
        cache_bias[:, window(turn)] = (
            1.0 - jnp.dot(hit, widen, preferred_element_type=jnp.float32)
        ) * NEG
        return carry

    lax.fori_loop(0, (lively + per - 1) // per, shift_cache, 0)

    def score_cache(turn, carry):
        at = window(turn, part)
        score(kept_k, at, cache_bias[:, at], near)
        return carry

    lax.fori_loop(0, turns, score_cache, 0)
    peak = jnp.max(best[...], axis=1, keepdims=True)
    peak_ref[...] = peak
    best[...] = jnp.broadcast_to(peak, best.shape)

    def weigh(values, at, base):
        tall, size = 64, at.size
        for r in range(0, best.shape[0], tall):
            top = best[r : r + tall, :]
            total = sums[r : r + tall, :]
            for i in range(0, size, LANES):
                lanes = pl.ds(pl.multiple_of(base + at.start + i, LANES), LANES)
                piece = jnp.exp2(held[r : r + tall, lanes] - top)
                total = total + piece
                light[r : r + tall, i : i + LANES] = piece.astype(light.dtype)
            sums[r : r + tall, :] = total
        acc_ref[...] += jnp.dot(
            light[:, :size], values[at, :], preferred_element_type=jnp.float32
        )

    def weigh_near(turn, carry):
        weigh(vs, window(turn), 0)
        return carry

    def weigh_cache(turn, carry):
        weigh(kept_v, window(turn, part), near)
        return carry

    lax.fori_loop(0, near // span, weigh_near, 0)
    lax.fori_loop(0, turns, weigh_cache, 0)
    whole_ref[...] = jnp.sum(sums[...], axis=1, keepdims=True)


def dense_part(spot, asked, cache_k, cache_v, blocks, near_k, near_v, ids, chosen, owned):
    width = asked[0].shape[1]
    heads = len(asked)
    rows = heads * asked[0].shape[0]
    steps = chosen.shape[0]
    far, near = cache_k.shape[0], near_k.shape[0]
    f32 = jnp.float32
    square = jax.ShapeDtypeStruct((rows, width), f32)
    span = min(2048, far, near)
    column = jax.ShapeDtypeStruct((rows, 1), f32)
    tile = pltpu.VMEM((rows, LANES), f32)
    return pl.pallas_call(
        functools.partial(
            dense_body, scale=width ** (-0.5) * LOG2E, steps=steps, span=span,
            block_len=far // blocks.shape[1], heads=heads,
        ),
        in_specs=smem(2) + vmem(heads + 7), out_specs=vmem(5),
        out_shape=[column, column, square, square, jax.ShapeDtypeStruct((steps, owned), f32)],
        scratch_shapes=[
            pltpu.VMEM((rows, width), asked[0].dtype), pltpu.VMEM((rows, far + near), f32), tile, tile,
            pltpu.VMEM((steps, far), f32), pltpu.VMEM((steps, blocks.shape[1]), f32),
            pltpu.VMEM((steps, near), f32), pltpu.VMEM((rows, span), jnp.bfloat16),
            pltpu.VMEM((far, width), cache_k.dtype), pltpu.VMEM((far, width), cache_v.dtype),
            pltpu.VMEM((2, blocks.shape[1]), jnp.int32), pltpu.SMEM((2, blocks.shape[1]), jnp.int32),
            pltpu.SemaphoreType.DMA(()),
        ],
        compiler_params=params(24),
        cost_estimate=cost(4 * rows * (far + near) * width),
        name="dense_part",
    )(*spot, *asked, cache_k, cache_v, blocks, near_k, near_v, ids, chosen)


def pieces_of(value, count):
    out = []
    for _ in range(count):
        piece = value.astype(jnp.bfloat16)
        out.append(piece)
        value = value - piece.astype(jnp.float32)
    return out


def finish_body(
    spot_ref, own_ref, *refs, owned, lines, steps, groups, scale, parcels
):
    came = refs[:parcels]
    (ck, cv, cc, bias_ref, q_ref, peak_ref, whole_ref, acc_ref,
     nk_ref, nv_ref, nc_ref, out_ref, res_ref, held) = refs[parcels:]
    width = ck.shape[1]
    sums = own_ref[:owned, :]
    tail = own_ref[owned:, :]
    for ref in came:
        sums = sums + ref[:owned, :].astype(jnp.float32)
        tail = tail + ref[owned:, :].astype(jnp.float32)
    pairs = 256.0 * tail[:, :LANES] + tail[:, LANES:]
    added = pairs[:lines] + pairs[lines : 2 * lines]
    old_row = cc[:, pl.ds(pl.multiple_of(spot_ref[0] * owned, owned), owned)]
    total_row = old_row + jnp.concatenate([added[i : i + 1] for i in range(lines)], axis=1)
    nc_ref[...] = total_row
    eye = lax.broadcasted_iota(jnp.int32, (LANES, LANES), 0) == lax.broadcasted_iota(
        jnp.int32, (LANES, LANES), 1
    )

    def stand(row):
        return jnp.sum(jnp.where(eye, row, 0.0), axis=1, keepdims=True)

    def column(row):
        return jnp.concatenate(
            [stand(row[:, i : i + LANES]) for i in range(0, owned, LANES)], axis=0
        )

    old_col, new_col = column(old_row), column(total_row)
    new_k = (old_col * ck[...] + sums[:, :width]) / new_col
    new_v = (old_col * cv[...] + sums[:, width:]) / new_col
    nk_ref[...] = new_k
    nv_ref[...] = new_v
    log_row = jnp.log(total_row) * LOG2E
    query = q_ref[...].astype(jnp.bfloat16)
    scores = sum(
        lax.dot_general(
            query, piece, (((1,), (1,)), ((), ())), preferred_element_type=jnp.float32
        )
        for piece in reversed(pieces_of(new_k, 3))
    )
    scores = scores * scale + log_row
    rows_all = scores.shape[0]
    rows = rows_all // steps
    shift = bias_ref[...]
    scores = jnp.concatenate(
        [scores[s * rows : (s + 1) * rows] + shift[s : s + 1] for s in range(steps)], axis=0
    )
    before = peak_ref[...]
    peak = jnp.maximum(before, jnp.max(scores, axis=1, keepdims=True))
    weights = jnp.exp2(scores - peak)
    fade = jnp.exp2(before - peak)
    whole = whole_ref[...] * fade + jnp.sum(weights, axis=1, keepdims=True)
    (w_high, w_low), (v_high, v_low) = pieces_of(weights, 2), pieces_of(new_v, 2)
    acc = acc_ref[...] * fade
    for left, right in ((w_low, v_high), (w_high, v_low), (w_high, v_high)):
        acc = acc + jnp.dot(left, right, preferred_element_type=jnp.float32)
    res_ref[...] = acc / whole
    level = peak + jnp.log(whole) * LOG2E
    marks = [
        jnp.sum(jnp.where(eye, level[i * LANES : (i + 1) * LANES], 0.0), axis=0, keepdims=True)
        for i in range(rows_all // LANES)
    ]
    marks = [piece.astype(jnp.float32) for mark in marks for piece in pieces_of(mark, 3)]
    marks = jnp.concatenate(marks + [jnp.zeros((TAIL - len(marks), LANES), jnp.float32)], axis=0)
    share = rows // groups
    for g in range(groups):
        for s in range(steps):
            held[g, s * share : (s + 1) * share, :] = res_ref[
                s * rows + g * share : s * rows + (g + 1) * share, :
            ]
        held[g, steps * share :, :] = marks
    out_ref[...] = held[...].astype(out_ref.dtype)


def finish(spot, own, came, cent_k, cent_v, counts, bias, query, dense, groups, owned):
    width = cent_k.shape[1]
    rows = query.shape[0]
    steps = bias.shape[0]
    lines = owned // LANES
    height = steps * (rows // steps // groups) + TAIL
    f32 = jnp.float32
    args = [spot[0], own, *came, cent_k, cent_v, counts, bias, query, *dense]
    return pl.pallas_call(
        functools.partial(
            finish_body, owned=owned, lines=lines, steps=steps, groups=groups,
            scale=width ** (-0.5) * LOG2E, parcels=len(came),
        ),
        in_specs=smem(1) + vmem(len(args) - 1), out_specs=vmem(4),
        scratch_shapes=[
            pltpu.VMEM((rows, width), f32), pltpu.VMEM((groups, height, LANES), f32),
        ],
        out_shape=[
            jax.ShapeDtypeStruct((owned, width), f32),
            jax.ShapeDtypeStruct((owned, width), f32),
            jax.ShapeDtypeStruct((1, owned), f32),
            jax.ShapeDtypeStruct((groups, height, LANES), jnp.bfloat16),
        ],
        compiler_params=params(16), cost_estimate=cost(4e9),
        name="finish",
    )(*args)


def blend_body(spot_ref, in_ref, out_ref, *, steps, share, groups, rows):
    count = steps * share
    tiles = steps * rows // LANES
    spot = lax.broadcasted_iota(jnp.int32, (count, LANES), 0)
    lane = lax.broadcasted_iota(jnp.int32, (count, LANES), 1)
    wanted = (spot // share) * rows + spot_ref[0] * share + spot % share
    picks = [wanted == lane + i * LANES for i in range(tiles)]
    levels = []
    for g in range(groups):
        level = jnp.zeros((count, LANES), jnp.float32)
        marks = in_ref[g, count:, :].astype(jnp.float32)
        for i in range(tiles):
            mark = marks[3 * i : 3 * i + 1] + marks[3 * i + 1 : 3 * i + 2] + marks[3 * i + 2 : 3 * i + 3]
            level = level + jnp.where(picks[i], mark, 0.0)
        levels.append(jnp.sum(level, axis=1, keepdims=True))
    top = functools.reduce(jnp.maximum, levels)
    parts = [jnp.exp2(level - top) for level in levels]
    whole = functools.reduce(jnp.add, parts)
    acc = sum(part * in_ref[g, :count, :].astype(jnp.float32) for g, part in enumerate(parts))
    out_ref[...] = (acc / whole).astype(out_ref.dtype)


def blend(spot, packets, steps, share, groups, rows):
    return pl.pallas_call(
        functools.partial(blend_body, steps=steps, share=share, groups=groups, rows=rows),
        in_specs=smem(1) + vmem(1), out_specs=vmem(1)[0],
        out_shape=jax.ShapeDtypeStruct((steps * share, LANES), jnp.bfloat16),
        compiler_params=params(8),
        name="blend",
    )(spot[0], packets)


def spread(pairs):
    return [(2 * a + core, 2 * b + core) for a, b in pairs for core in (0, 1)]


def shards(
    stretch_keys, stretch_values, stretch_assign, centroid_keys, centroid_values, cluster_counts,
    cache_keys, cache_values, block_cluster, selected, queries,
):
    clusters, width = centroid_keys.shape[1:]
    groups = lax.axis_size("ctx")
    owned = clusters // groups
    chips = groups // 2
    swap = [(i, i ^ 1) for i in range(groups)]
    spot = tuple(lax.axis_index(name).astype(jnp.int32).reshape(1) for name in ("ctx", "head"))

    mine = (stretch_keys[0], stretch_values[0], stretch_assign)
    other = tuple(lax.ppermute(a, "ctx", swap) for a in mine)
    lead = 3 if chips == 4 else 1
    slot_a = segment_sums(spot, lead, chips, (mine,), None, None, owned, jnp.float32)
    counts = chip_counts(mine[2], other[2], clusters)
    slot_a = segment_sums(spot, lead, chips, (other,), slot_a, counts, owned, jnp.bfloat16)

    def sums_for(turn):
        return segment_sums(spot, turn, chips, (mine, other), None, counts, owned, jnp.bfloat16)

    def move(a, pairs):
        return lax.ppermute(a, "ctx", spread(pairs))

    if chips == 4:
        first = move(slot_a, [(0, 1), (3, 2)])
        across = move(slot_a, [(1, 2), (2, 1)])
        slot_b = sums_for(2)
        skip = move(slot_b, [(0, 2), (3, 1)])
        passed = relay(slot_b, first, owned)
        far = move(passed, [(1, 3), (2, 0)])
        slot_c = sums_for(1)
        beside = move(slot_c, [(0, 1), (1, 0), (2, 3), (3, 2)])
        came = [skip, across, beside, far]
    else:
        came = [move(slot_a, [(i, (i + 1) % chips) for i in range(chips)])]
        for d in range(2, chips):
            slot = sums_for(d)
            came.append(move(slot, [(i, (i + d) % chips) for i in range(chips)]))
    own, own_k, own_v = home_sums(
        spot, chips, mine, other, counts, centroid_keys[0], centroid_values[0], owned
    )
    heads = lax.axis_size("head")
    asked = list(by_head(spot, queries))
    for d in range(1, heads):
        asked[d] = lax.ppermute(asked[d], "head", [(i, (i + d) % heads) for i in range(heads)])
    steps = queries.shape[0]
    query_rows = heads * queries.shape[1]
    *dense, query, own_bias = dense_part(
        spot, asked, cache_keys[0], cache_values[0],
        block_cluster, *mine, selected[:, 0], owned,
    )
    new_keys, new_values, new_counts, packets = finish(
        spot, own, came, own_k, own_v, cluster_counts,
        own_bias, query, dense, groups, owned,
    )
    packets = lax.all_to_all(packets, "ctx", split_axis=0, concat_axis=0, tiled=True)
    share = query_rows // groups
    result = blend(spot, packets, steps, share, groups, query_rows)
    return (
        new_keys[None],
        new_values[None],
        new_counts,
        result.reshape(steps, 1, share, width),
    )


def solution(mesh):
    in_specs = (
        P("head", "ctx", None),
        P("head", "ctx", None),
        P("head", "ctx"),
        P("head", None, None),
        P("head", None, None),
        P("head", None),
        P("head", "ctx", None),
        P("head", "ctx", None),
        P("head", "ctx"),
        P(None, "head", None),
        P(None, "head", None, None),
    )
    out_specs = (
        P("head", "ctx", None),
        P("head", "ctx", None),
        P("head", "ctx"),
        P(None, "head", "ctx", None),
    )
    return jax.shard_map(shards, mesh=mesh, in_specs=in_specs, out_specs=out_specs, check_vma=False)
```

time: 58 us -> 54.3 us (0.936)
  Pallas kernels: 20.9 us -> 17.6 us
  waiting for transfers between devices: 1.37 us -> 4.38 us
  blocking collectives: 10.5 us -> 9.24 us
  starting transfers between devices: 18.7 us -> 17.6 us
  local copies, waits for them, and re-layouts: 5.14 us -> 4.09 us
    pallas_call x1, Pallas kernels: 7.75 us -> 4.45 us  [dense_part(): pl.pallas_call(functools.partial(dense_body, scale=width ** (-0.5) * LOG2...]
    ppermute x5, waiting for transfers between devices: 1.35 us -> 4.37 us  [move(): return lax.ppermute(a, 'ctx', spread(pairs))]
    pallas_call x0 -> x1, Pallas kernels: none -> 2.4 us  [home_sums(): pl.pallas_call(functools.partial(home_body, owned=owned, turn=0, chips=ch...]
    pallas_call x5 -> x4, Pallas kernels: 9.49 us -> 7.16 us  [segment_sums(): pl.pallas_call(functools.partial(segment_body, owned=owned, sources=len(s...]
    ppermute x5, starting transfers between devices: 12.9 us -> 10.9 us  [move(): return lax.ppermute(a, 'ctx', spread(pairs))]
    all_to_all x1, blocking collectives: 10.5 us -> 9.24 us  [shards(): lax.all_to_all(packets, 'ctx', split_axis=0, concat_axis=0, tiled=True)]
    dynamic_slice x2 -> x0, local copies, waits for them, and re-layouts: 1.07 us -> none  [the longest x1 1.06 us: shards(): lax.dynamic_slice_in_dim(centroid_values[0], me * owned, owned, 0)]
    ppermute x3, starting transfers between devices: 4.73 us -> 5.61 us  [shards(): lax.ppermute(asked[d], 'head', [(i, (i + d) % heads) for i in range(heads)])]
  transfers between devices with their start and end apart: 11 -> 11, of which waited for: 1 -> 1; matrix products, arithmetic and copies ran while one was open for 2% -> 0% of each run, Pallas kernels for 31% -> 28%
where the time goes in v1:
time: 54.3 us; the launch traced here: 53.9 us
  starting transfers between devices  17.6 us (32%)
  Pallas kernels  17.6 us (32%)
  blocking collectives  9.24 us (17%)
  waiting for transfers between devices  4.38 us (8%)
  local copies, waits for them, and re-layouts  4.09 us (8%)
  between operations  0.93 us (2%)
    ppermute x5, starting transfers between devices, move(): return lax.ppermute(a, 'ctx', spread(pairs))  10.9 us
    all_to_all x1, blocking collectives, shards(): lax.all_to_all(packets, 'ctx', split_axis=0, concat_axis=0, tiled=True)  9.24 us
    pallas_call x4, Pallas kernels, segment_sums(): pl.pallas_call(functools.partial(segment_body, owned=owned, sources=len(s...  7.16 us
    ppermute x3, starting transfers between devices, shards(): lax.ppermute(asked[d], 'head', [(i, (i + d) % heads) for i in range(heads)])  5.61 us
    pallas_call x1, Pallas kernels, dense_part(): pl.pallas_call(functools.partial(dense_body, scale=width ** (-0.5) * LOG2...  4.45 us
    ppermute x5, waiting for transfers between devices, move(): return lax.ppermute(a, 'ctx', spread(pairs))  4.37 us
    unnamed x28, local copies, waits for them, and re-layouts  4.09 us
    pallas_call x1, Pallas kernels, home_sums(): pl.pallas_call(functools.partial(home_body, owned=owned, turn=0, chips=ch...  2.4 us
  transfers between devices with their start and end apart: 11, of which 1 were waited for; matrix products, arithmetic and copies ran while one was open for 0% of the time, Pallas kernels for 28%

profile of v1, /device:TPU:0, one launch (start us, length us, event | category | flops | bytes accessed | tf_op | source)
XLA Modules:
  0.0 53.9 jit_solution(16000890462329207095)
XLA Ops:
  0.6 0.6 %collective-permute-start = (bf16[4096,128]{1,0:T(8,128)(2,1)}, bf16[4096,128]{1,0:T(8,128)(2,1)S(1)}, u32[]{:S(2)}, u32[]{:S(2)}) collective-permute-start(bf16[4096,128]{1,0:T(8,128)(2,1)} %bitcast.16), channel_id=1, source_target_pairs={{0,4},{4,0},{8,12},{12,8},{16,20},{20,16},{24,28},{28,24},{1,5},{5... | collective-permute-start | bytes 3145736 | tf_op jit(solution)/shard_map/ppermute | solution.py:584
  1.2 0.1 collective-permute-start.1
  1.3 0.4 collective-permute-start.2
  1.7 0.8 %copy-done.12 = bf16[4,16,4,128]{3,2,1,0:T(4,128)(2,1)S(1)} copy-done((bf16[4,16,4,128]{3,2,1,0:T(4,128)(2,1)S(1)}, bf16[4,16,4,128]{3,2,1,0:T(4,128)(2,1)}, u32[]{:S(2)}) %copy-start.12) | copy-done | bytes 65560
  2.6 2.6 %collective-permute-start.8 = (bf16[64,128]{1,0:T(8,128)(2,1)S(1)}, bf16[64,128]{1,0:T(8,128)(2,1)S(1)}, u32[]{:S(2)}, u32[]{:S(2)}) collective-permute-start(bf16[64,128]{1,0:T(8,128)(2,1)S(1)} %get-tuple-element.24), channel_id=1, source_target_pairs={{0,1},{1,2},{2,3},{3,0},{4,5},{5,6},{6,7},{7,4},{8,9},{9,10},{10,1... | collective-permute-start | bytes 49160 | tf_op jit(solution)/shard_map/ppermute | solution.py:617
  5.2 1.5 %collective-permute-start.9 = (bf16[64,128]{1,0:T(8,128)(2,1)S(1)}, bf16[64,128]{1,0:T(8,128)(2,1)S(1)}, u32[]{:S(2)}, u32[]{:S(2)}) collective-permute-start(bf16[64,128]{1,0:T(8,128)(2,1)S(1)} %get-tuple-element.25), channel_id=1, source_target_pairs={{0,2},{1,3},{2,0},{3,1},{4,6},{5,7},{6,4},{7,5},{8,10},{9,11},{10,... | collective-permute-start | bytes 49160 | tf_op jit(solution)/shard_map/ppermute | solution.py:617
  6.7 1.2 %copy-done = bf16[1,4096,128]{2,1,0:T(8,128)(2,1)S(1)} copy-done((bf16[1,4096,128]{2,1,0:T(8,128)(2,1)S(1)}, bf16[1,4096,128]{2,1,0:T(8,128)(2,1)}, u32[]{:S(2)}) %copy-start) | copy-done | bytes 1048600
  7.9 1.2 %copy-done.2 = bf16[1,4096,128]{2,1,0:T(8,128)(2,1)S(1)} copy-done((bf16[1,4096,128]{2,1,0:T(8,128)(2,1)S(1)}, bf16[1,4096,128]{2,1,0:T(8,128)(2,1)}, u32[]{:S(2)}) %copy-start.2) | copy-done | bytes 1048600
  9.2 0.7 %copy-done.8 = s32[1,4096]{1,0:T(1,128)S(1)} copy-done((s32[1,4096]{1,0:T(1,128)S(1)}, s32[1,4096]{1,0:T(1,128)}, u32[]{:S(2)}) %copy-start.8) | copy-done | bytes 16408
  9.9 1.2 %shard_map.139.refs_3_ = f32[512,256]{1,0:T(8,128)S(1)} custom-call(s32[1]{0:T(128)} %bitcast.spot_ref, s32[1]{0:T(128)} %bitcast.6.head_ref, bf16[4096,128]{1,0:T(8,128)(2,1)S(1)} %bitcast.17, bf16[4096,128]{1,0:T(8,128)(2,1)S(1)} %bitcast.23, s32[1,4096]{1,0:T(1,128)S(1)} %copy-done.8), custom_call_target="tpu_custom_call" | custom-call | flops 1073741824 | bytes 1048576 | tf_op jit(solution)/shard_map/pallas_call | solution.py:134
  11.1 1.5 %collective-permute-start.10 = (bf16[64,128]{1,0:T(8,128)(2,1)S(1)}, bf16[64,128]{1,0:T(8,128)(2,1)S(1)}, u32[]{:S(2)}, u32[]{:S(2)}) collective-permute-start(bf16[64,128]{1,0:T(8,128)(2,1)S(1)} %get-tuple-element.26), channel_id=1, source_target_pairs={{0,3},{1,0},{2,1},{3,2},{4,7},{5,4},{6,5},{7,6},{8,11},{9,8},{10,9... | collective-permute-start | bytes 49160 | tf_op jit(solution)/shard_map/ppermute | solution.py:617
  12.6 0.8 %chip_counts.1 = f32[32,128]{1,0:T(8,128)S(1)} custom-call(s32[1,4096]{1,0:T(1,128)S(1)} %copy-done.8, s32[1,4096]{1,0:T(1,128)S(1)} %collective-permute-done.2.other_ref.refs_5_.refs_2_), custom_call_target="tpu_custom_call" | custom-call | flops 1000000000 | bytes 1048576 | tf_op jit(solution)/shard_map/chip_counts/pallas_call | solution.py:77
  13.4 0.0 copy-start.3
  13.5 1.3 %shard_map.140 = bf16[528,256]{1,0:T(8,128)(2,1)S(1)} custom-call(s32[1]{0:T(128)} %bitcast.spot_ref, s32[1]{0:T(128)} %bitcast.6.head_ref, bf16[4096,128]{1,0:T(8,128)(2,1)S(1)} %collective-permute-done.refs_3_.refs_0_, bf16[4096,128]{1,0:T(8,128)(2,1)S(1)} %collective-permute-done.1.refs_4_.refs_1_, ...), custom_call_target="tpu_custom_call" | custom-call | flops 1073741824 | bytes 1048576 | tf_op jit(solution)/shard_map/pallas_call | solution.py:134
  14.7 3.5 %collective-permute-start.6 = (bf16[528,256]{1,0:T(8,128)(2,1)S(1)}, bf16[528,256]{1,0:T(8,128)(2,1)S(1)}, u32[]{:S(2)}, u32[]{:S(2)}) collective-permute-start(bf16[528,256]{1,0:T(8,128)(2,1)S(1)} %shard_map.140), channel_id=1, source_target_pairs={{0,8},{4,12},{24,16},{28,20},{1,9},{5,13},{25,17},{29,21},{2,10},{... | collective-permute-start | bytes 811016 | tf_op jit(solution)/shard_map/ppermute | solution.py:594
  18.2 0.7 %collective-permute-start.4 = (bf16[528,256]{1,0:T(8,128)(2,1)S(1)}, bf16[528,256]{1,0:T(8,128)(2,1)S(1)}, u32[]{:S(2)}, u32[]{:S(2)}) collective-permute-start(bf16[528,256]{1,0:T(8,128)(2,1)S(1)} %shard_map.140), channel_id=1, source_target_pairs={{8,16},{12,20},{16,8},{20,12},{9,17},{13,21},{17,9},{21,13},{10,18... | collective-permute-start | bytes 811016 | tf_op jit(solution)/shard_map/ppermute | solution.py:594
  19.0 2.3 %shard_map.138.own_ref = bf16[528,256]{1,0:T(8,128)(2,1)S(1)} custom-call(s32[1]{0:T(128)} %bitcast.spot_ref, s32[1]{0:T(128)} %bitcast.6.head_ref, bf16[4096,128]{1,0:T(8,128)(2,1)S(1)} %bitcast.18, bf16[4096,128]{1,0:T(8,128)(2,1)S(1)} %bitcast.24, s32[1,4096]{1,0:T(1,128)S(1)} %copy-done.9, bf16[4096,128]{1,0:T(8,128)(2,1)S(1)} %collective-permute-done.refs_3_.refs_0_, ...), custom_call_target="tpu_custom_call" | custom-call | flops 2147483648 | bytes 1048576 | tf_op jit(solution)/shard_map/pallas_call | solution.py:134
  21.3 2.3 %shard_map.141 = bf16[528,256]{1,0:T(8,128)(2,1)S(1)} custom-call(s32[1]{0:T(128)} %bitcast.spot_ref, s32[1]{0:T(128)} %bitcast.6.head_ref, bf16[4096,128]{1,0:T(8,128)(2,1)S(1)} %bitcast.19, bf16[4096,128]{1,0:T(8,128)(2,1)S(1)} %bitcast.25, s32[1,4096]{1,0:T(1,128)S(1)} %copy-done.9, bf16[4096,128]{1,0:T(8,128)(2,1)S(1)} %collective-permute-done.refs_3_.refs_0_, ...), custom_call_target="tpu_custom_call" | custom-call | flops 2147483648 | bytes 1048576 | tf_op jit(solution)/shard_map/pallas_call | solution.py:134
  23.6 0.0 copy-start.4
  23.7 0.0 collective-permute-done.6.came_ref
  23.7 5.4 %collective-permute-start.3 = (bf16[528,256]{1,0:T(8,128)(2,1)S(1)}, bf16[528,256]{1,0:T(8,128)(2,1)S(1)}, u32[]{:S(2)}, u32[]{:S(2)}) collective-permute-start(bf16[528,256]{1,0:T(8,128)(2,1)S(1)} %shard_map.138.own_ref), channel_id=1, source_target_pairs={{0,16},{4,20},{24,8},{28,12},{1,17},{5,21},{25,9},{29,13},{2,18},{... | collective-permute-start | bytes 811016 | tf_op jit(solution)/shard_map/ppermute | solution.py:594
  29.1 0.1 relay.1
  29.2 0.1 collective-permute-start.5
  29.3 1.3 %collective-permute-start.7 = (bf16[528,256]{1,0:T(8,128)(2,1)S(1)}, bf16[528,256]{1,0:T(8,128)(2,1)S(1)}, u32[]{:S(2)}, u32[]{:S(2)}) collective-permute-start(bf16[528,256]{1,0:T(8,128)(2,1)S(1)} %relay.1), channel_id=1, source_target_pairs={{8,24},{12,28},{16,0},{20,4},{9,25},{13,29},{17,1},{21,5},{10,26},... | collective-permute-start | bytes 811016 | tf_op jit(solution)/shard_map/ppermute | solution.py:594
  30.6 0.0 copy-start.6
  30.7 0.0 copy-start.7
  30.7 4.4 %dense_part.1 = (f32[256,1]{1,0:T(8,128)S(1)}, f32[256,1]{1,0:T(8,128)S(1)}, f32[256,128]{1,0:T(8,128)S(1)}, f32[256,128]{1,0:T(8,128)S(1)}, f32[4,512]{1,0:T(4,128)S(1)}) custom-call(s32[1]{0:T(128)} %bitcast.spot_ref, s32[1]{0:T(128)} %bitcast.6.head_ref, bf16[64,128]{1,0:T(8,128)(2,1)S(1)} %get-tuple-element.23.refs_0_, ...), custom_call_target="tpu_custom_call" | custom-call | flops 1610612736 | bytes 1048576 | tf_op jit(solution)/shard_map/dense_part/pallas_call | solution.py:402
  35.2 2.4 %home_sums.1 = (f32[528,256]{1,0:T(8,128)S(1)}, f32[512,128]{1,0:T(8,128)S(1)}, f32[512,128]{1,0:T(8,128)S(1)}) custom-call(s32[1]{0:T(128)} %bitcast.spot_ref, f32[4096,128]{1,0:T(8,128)S(1)} %bitcast.30, f32[4096,128]{1,0:T(8,128)S(1)} %bitcast.31, bf16[4096,128]{1,0:T(8,128)(2,1)S(1)} %bitcast.21, bf16[4096,128]{1,0:T(8,128)(2,1)S(1)} %bitcast.27, ...), custom_call_target="tpu_custom_call" | custom-call | flops 2147483648 | bytes 1048576 | tf_op jit(solution)/shard_map/home_sums/pallas_call | solution.py:167
  37.6 4.3 %collective-permute-done.5.refs_2_ = bf16[528,256]{1,0:T(8,128)(2,1)S(1)} collective-permute-done((bf16[528,256]{1,0:T(8,128)(2,1)S(1)}, bf16[528,256]{1,0:T(8,128)(2,1)S(1)}, u32[]{:S(2)}, u32[]{:S(2)}) %collective-permute-start.5) | collective-permute-done | bytes 270368 | tf_op jit(solution)/shard_map/ppermute | solution.py:594
  41.9 2.0 %finish.1 = (f32[512,128]{1,0:T(8,128)}, f32[512,128]{1,0:T(8,128)}, f32[1,512]{1,0:T(1,128)}, bf16[8,48,128]{2,1,0:T(8,128)(2,1)S(1)}) custom-call(s32[1]{0:T(128)} %bitcast.spot_ref, f32[528,256]{1,0:T(8,128)S(1)} %get-tuple-element.20.own_ref, bf16[528,256]{1,0:T(8,128)(2,1)S(1)} %collective-permute-done.3.refs_0_, ...), custom_call_target="tpu_custom_call" | custom-call | flops 4000000000 | bytes 1048576 | tf_op jit(solution)/shard_map/finish/pallas_call | solution.py:516
  43.9 9.2 %all_to_all.5.in_ref = bf16[8,48,128]{2,1,0:T(8,128)(2,1)S(1)} all-to-all(bf16[8,48,128]{2,1,0:T(8,128)(2,1)S(1)} %get-tuple-element.35), channel_id=1, replica_groups=mesh['ctx'=8,'head'=4] {'ctx'}, dimensions={0} | all-to-all | bytes 196608 | tf_op jit(solution)/shard_map/all_to_all | solution.py:628
  53.1 0.7 %blend.1 = bf16[32,128]{1,0:T(8,128)(2,1)} custom-call(s32[1]{0:T(128)} %bitcast.spot_ref, bf16[8,48,128]{2,1,0:T(8,128)(2,1)S(1)} %all_to_all.5.in_ref), custom_call_target="tpu_custom_call" | custom-call | tf_op jit(solution)/shard_map/blend/pallas_call | solution.py:559
  (30 shorter events, 0.1 us)
Async XLA Ops:
  0.6 12.8 %collective-permute-start = (bf16[4096,128]{1,0:T(8,128)(2,1)}, bf16[4096,128]{1,0:T(8,128)(2,1)S(1)}, u32[]{:S(2)}, u32[]{:S(2)}) collective-permute-start(bf16[4096,128]{1,0:T(8,128)(2,1)} %bitcast.16), channel_id=1, source_target_pairs={{0,4},{4,0},{8,12},{12,8},{16,20},{20,16},{24,28},{28,24},{1,5},{5... | collective-permute-start | bytes 3145736 | tf_op jit(solution)/shard_map/ppermute | solution.py:584
  1.2 12.3 %collective-permute-start.1 = (bf16[4096,128]{1,0:T(8,128)(2,1)}, bf16[4096,128]{1,0:T(8,128)(2,1)S(1)}, u32[]{:S(2)}, u32[]{:S(2)}) collective-permute-start(bf16[4096,128]{1,0:T(8,128)(2,1)} %bitcast.22), channel_id=1, source_target_pairs={{0,4},{4,0},{8,12},{12,8},{16,20},{20,16},{24,28},{28,24},{1,5},{5... | collective-permute-start | bytes 3145736 | tf_op jit(solution)/shard_map/ppermute | solution.py:584
  1.3 9.9 %collective-permute-start.2 = (s32[1,4096]{1,0:T(1,128)}, s32[1,4096]{1,0:T(1,128)S(1)}, u32[]{:S(2)}, u32[]{:S(2)}) collective-permute-start(s32[1,4096]{1,0:T(1,128)} %refs_9_.1), channel_id=1, source_target_pairs={{0,4},{4,0},{8,12},{12,8},{16,20},{20,16},{24,28},{28,24},{1,5},{5... | collective-permute-start | bytes 49160 | tf_op jit(solution)/shard_map/ppermute | solution.py:584
  1.7 0.8 %copy-start.12 = (bf16[4,16,4,128]{3,2,1,0:T(4,128)(2,1)S(1)}, bf16[4,16,4,128]{3,2,1,0:T(4,128)(2,1)}, u32[]{:S(2)}) copy-start(bf16[4,16,4,128]{3,2,1,0:T(4,128)(2,1)} %param.21) | copy-start | bytes 196612
  2.6 26.6 %collective-permute-start.8 = (bf16[64,128]{1,0:T(8,128)(2,1)S(1)}, bf16[64,128]{1,0:T(8,128)(2,1)S(1)}, u32[]{:S(2)}, u32[]{:S(2)}) collective-permute-start(bf16[64,128]{1,0:T(8,128)(2,1)S(1)} %get-tuple-element.24), channel_id=1, source_target_pairs={{0,1},{1,2},{2,3},{3,0},{4,5},{5,6},{6,7},{7,4},{8,9},{9,10},{10,1... | collective-permute-start | bytes 49160 | tf_op jit(solution)/shard_map/ppermute | solution.py:617
  5.2 24.1 %collective-permute-start.9 = (bf16[64,128]{1,0:T(8,128)(2,1)S(1)}, bf16[64,128]{1,0:T(8,128)(2,1)S(1)}, u32[]{:S(2)}, u32[]{:S(2)}) collective-permute-start(bf16[64,128]{1,0:T(8,128)(2,1)S(1)} %get-tuple-element.25), channel_id=1, source_target_pairs={{0,2},{1,3},{2,0},{3,1},{4,6},{5,7},{6,4},{7,5},{8,10},{9,11},{10,... | collective-permute-start | bytes 49160 | tf_op jit(solution)/shard_map/ppermute | solution.py:617
  6.7 1.2 %copy-start = (bf16[1,4096,128]{2,1,0:T(8,128)(2,1)S(1)}, bf16[1,4096,128]{2,1,0:T(8,128)(2,1)}, u32[]{:S(2)}) copy-start(bf16[1,4096,128]{2,1,0:T(8,128)(2,1)} %param.11) | copy-start | bytes 3145732
  7.9 1.2 %copy-start.2 = (bf16[1,4096,128]{2,1,0:T(8,128)(2,1)S(1)}, bf16[1,4096,128]{2,1,0:T(8,128)(2,1)}, u32[]{:S(2)}) copy-start(bf16[1,4096,128]{2,1,0:T(8,128)(2,1)} %param.12) | copy-start | bytes 3145732
  9.1 0.7 %copy-start.8 = (s32[1,4096]{1,0:T(1,128)S(1)}, s32[1,4096]{1,0:T(1,128)}, u32[]{:S(2)}) copy-start(s32[1,4096]{1,0:T(1,128)} %refs_9_.1) | copy-start | bytes 49156
  11.1 19.5 %collective-permute-start.10 = (bf16[64,128]{1,0:T(8,128)(2,1)S(1)}, bf16[64,128]{1,0:T(8,128)(2,1)S(1)}, u32[]{:S(2)}, u32[]{:S(2)}) collective-permute-start(bf16[64,128]{1,0:T(8,128)(2,1)S(1)} %get-tuple-element.26), channel_id=1, source_target_pairs={{0,3},{1,0},{2,1},{3,2},{4,7},{5,4},{6,5},{7,6},{8,11},{9,8},{10,9... | collective-permute-start | bytes 49160 | tf_op jit(solution)/shard_map/ppermute | solution.py:617
  13.4 5.5 %copy-start.1 = (bf16[1,4096,128]{2,1,0:T(8,128)(2,1)S(1)}, bf16[1,4096,128]{2,1,0:T(8,128)(2,1)}, u32[]{:S(2)}) copy-start(bf16[1,4096,128]{2,1,0:T(8,128)(2,1)} %param.11) | copy-start | bytes 3145732
  13.4 5.5 %copy-start.3 = (bf16[1,4096,128]{2,1,0:T(8,128)(2,1)S(1)}, bf16[1,4096,128]{2,1,0:T(8,128)(2,1)}, u32[]{:S(2)}) copy-start(bf16[1,4096,128]{2,1,0:T(8,128)(2,1)} %param.12) | copy-start | bytes 3145732
  13.4 5.5 %copy-start.9 = (s32[1,4096]{1,0:T(1,128)S(1)}, s32[1,4096]{1,0:T(1,128)}, u32[]{:S(2)}) copy-start(s32[1,4096]{1,0:T(1,128)} %refs_9_.1) | copy-start | bytes 49156
  14.7 9.0 %collective-permute-start.6 = (bf16[528,256]{1,0:T(8,128)(2,1)S(1)}, bf16[528,256]{1,0:T(8,128)(2,1)S(1)}, u32[]{:S(2)}, u32[]{:S(2)}) collective-permute-start(bf16[528,256]{1,0:T(8,128)(2,1)S(1)} %shard_map.140), channel_id=1, source_target_pairs={{0,8},{4,12},{24,16},{28,20},{1,9},{5,13},{25,17},{29,21},{2,10},{... | collective-permute-start | bytes 811016 | tf_op jit(solution)/shard_map/ppermute | solution.py:594
  18.2 23.7 %collective-permute-start.4 = (bf16[528,256]{1,0:T(8,128)(2,1)S(1)}, bf16[528,256]{1,0:T(8,128)(2,1)S(1)}, u32[]{:S(2)}, u32[]{:S(2)}) collective-permute-start(bf16[528,256]{1,0:T(8,128)(2,1)S(1)} %shard_map.140), channel_id=1, source_target_pairs={{8,16},{12,20},{16,8},{20,12},{9,17},{13,21},{17,9},{21,13},{10,18... | collective-permute-start | bytes 811016 | tf_op jit(solution)/shard_map/ppermute | solution.py:594
  21.3 9.3 %copy-start.5 = (bf16[1,8192,128]{2,1,0:T(8,128)(2,1)S(1)}, bf16[1,8192,128]{2,1,0:T(8,128)(2,1)}, u32[]{:S(2)}) copy-start(bf16[1,8192,128]{2,1,0:T(8,128)(2,1)} %param.18) | copy-start | bytes 6291460
  23.6 7.0 %copy-start.4 = (bf16[1,8192,128]{2,1,0:T(8,128)(2,1)S(1)}, bf16[1,8192,128]{2,1,0:T(8,128)(2,1)}, u32[]{:S(2)}) copy-start(bf16[1,8192,128]{2,1,0:T(8,128)(2,1)} %param.17) | copy-start | bytes 6291460
  23.7 7.0 %copy-start.10 = (s32[1,512]{1,0:T(1,128)S(1)}, s32[1,512]{1,0:T(1,128)}, u32[]{:S(2)}) copy-start(s32[1,512]{1,0:T(1,128)} %refs_6_.2) | copy-start | bytes 6148
  23.7 7.0 %copy-start.11 = (s32[4,1,64]{2,1,0:T(1,128)S(1)}, s32[4,1,64]{2,1,0:T(1,128)}, u32[]{:S(2)}) copy-start(s32[4,1,64]{2,1,0:T(1,128)} %param.20) | copy-start | bytes 3076
  23.7 18.2 %collective-permute-start.3 = (bf16[528,256]{1,0:T(8,128)(2,1)S(1)}, bf16[528,256]{1,0:T(8,128)(2,1)S(1)}, u32[]{:S(2)}, u32[]{:S(2)}) collective-permute-start(bf16[528,256]{1,0:T(8,128)(2,1)S(1)} %shard_map.138.own_ref), channel_id=1, source_target_pairs={{0,16},{4,20},{24,8},{28,12},{1,17},{5,21},{25,9},{29,13},{2,18},{... | collective-permute-start | bytes 811016 | tf_op jit(solution)/shard_map/ppermute | solution.py:594
  29.2 12.7 %collective-permute-start.5 = (bf16[528,256]{1,0:T(8,128)(2,1)S(1)}, bf16[528,256]{1,0:T(8,128)(2,1)S(1)}, u32[]{:S(2)}, u32[]{:S(2)}) collective-permute-start(bf16[528,256]{1,0:T(8,128)(2,1)S(1)} %shard_map.141), channel_id=1, source_target_pairs={{0,8},{4,12},{8,0},{12,4},{16,24},{20,28},{24,16},{28,20},{1,9},{5... | collective-permute-start | bytes 811016 | tf_op jit(solution)/shard_map/ppermute | solution.py:594
  29.3 12.6 %collective-permute-start.7 = (bf16[528,256]{1,0:T(8,128)(2,1)S(1)}, bf16[528,256]{1,0:T(8,128)(2,1)S(1)}, u32[]{:S(2)}, u32[]{:S(2)}) collective-permute-start(bf16[528,256]{1,0:T(8,128)(2,1)S(1)} %relay.1), channel_id=1, source_target_pairs={{8,24},{12,28},{16,0},{20,4},{9,25},{13,29},{17,1},{21,5},{10,26},... | collective-permute-start | bytes 811016 | tf_op jit(solution)/shard_map/ppermute | solution.py:594
  30.6 4.5 %copy-start.6 = (f32[1,4096,128]{2,1,0:T(8,128)S(1)}, f32[1,4096,128]{2,1,0:T(8,128)}, u32[]{:S(2)}) copy-start(f32[1,4096,128]{2,1,0:T(8,128)} %param.14) | copy-start | bytes 6291460
  30.7 4.5 %copy-start.7 = (f32[1,4096,128]{2,1,0:T(8,128)S(1)}, f32[1,4096,128]{2,1,0:T(8,128)}, u32[]{:S(2)}) copy-start(f32[1,4096,128]{2,1,0:T(8,128)} %param.15) | copy-start | bytes 6291460
  35.1 6.8 %copy-start.13 = (f32[1,4096]{1,0:T(1,128)S(1)}, f32[1,4096]{1,0:T(1,128)}, u32[]{:S(2)}) copy-start(f32[1,4096]{1,0:T(1,128)} %refs_6_.3) | copy-start | bytes 49156
